TPU v7x, 256 devices: a whole 4x4x8 slice. The times are simulated.
256 devices in a mesh: tile: 32 (over y, z), grp: 8 (over x, core).
Axes of the slice: x: 4, y: 4, z: 8, core: 2. Of those that a mesh axis runs over, the one named last changes fastest.
Arguments:
- basis: float32 [131072, 2401], P(('tile', 'grp')), may hold values from -6 to 6
- pixel_ids: int32 [2097152], P(('tile', 'grp')), may hold values from 0 to 511
- band_ids: int32 [2097152], P(('tile', 'grp')), may hold values from 0 to 4
- mags: float32 [2097152], P(('tile', 'grp')), may hold values from -6 to 6
- inv_var: float32 [2097152], P(('tile', 'grp')), may hold values from 0.01 to 10
Outputs:
- solution: float32 [5, 2401], replicated
- residual: float32 [5, 2401], replicated
All inputs are finite; a program needn't handle non-finite values.
Results may differ from a plain program's by a relative error of at most 0.0003.
Values sent between devices are 32-bit elements; how exact they have to be, the bound alone decides.
No kernel may reach another device: no remote copies, remote signals or barrier semaphores. Data moves between devices by JAX's collectives and lax.ppermute only.
A program may use at most 64 MiB of HBM per device.

v0:
```python
import jax
import jax.numpy as jnp
from jax import lax
from jax.sharding import Mesh
from jax.sharding import PartitionSpec as P

BANDS = 5
ITERS = 3
TILE = ("tile_0", "tile_1")
GRP = ("grp_0", "grp_1")
TILE_GRP = ("tile_0", "tile_1", "grp_0", "grp_1")


ridge = 0.1


def filled_up(lines, size):
    spare = -len(lines) % size
    return jnp.pad(lines, [(0, spare)] + [(0, 0)] * (lines.ndim - 1))


def copy_for_each(array, axis):
    size = lax.axis_size(axis)
    return lax.all_to_all(
        jnp.broadcast_to(array[None], (size, *array.shape)), axis, 0, 0, tiled=True
    )


def in_order(parts, dim):
    parts = jnp.moveaxis(parts, 0, dim)
    shape = parts.shape
    return parts.reshape(*shape[:dim], shape[dim] * shape[dim + 1], *shape[dim + 2 :])


def gathered_by_axis(array, axes, dim):
    far, near = axes
    parts = copy_for_each(copy_for_each(array, far), near)
    return in_order(parts.swapaxes(0, 1).reshape(-1, *array.shape), dim)


def split_up(array, dim, size):
    shape = array.shape
    parts = array.reshape(*shape[:dim], size, shape[dim] // size, *shape[dim + 1 :])
    return jnp.moveaxis(parts, dim, 0)


def sum_at_owner(array, axis, dim):
    size = lax.axis_size(axis)
    parts = lax.all_to_all(split_up(array, dim, size), axis, 0, 0, tiled=True)
    return jnp.sum(parts, axis=0)


def summed_rows(array, axes, dim):
    far, near = axes
    own = sum_at_owner(split_up(array, dim, lax.axis_size(far)), near, dim + 1)
    return jnp.sum(lax.all_to_all(own, far, 0, 0, tiled=True), axis=0)


def nested_sum(array, axes):
    lines = array.reshape(-1)
    padded = filled_up(lines, lax.axis_size(axes[0]) * lax.axis_size(axes[1]))
    whole = gathered_by_axis(summed_rows(padded, axes, 0), axes, 0)
    return lax.slice_in_dim(whole, 0, len(lines)).reshape(array.shape)


def body(basis, pixel_ids, band_ids, mags, inv_var):
    pixels = basis.shape[0]
    total_pix = pixels * lax.axis_size(TILE) * lax.axis_size(GRP)
    segment = band_ids * pixels + pixel_ids
    counts = jax.ops.segment_sum(inv_var, segment, num_segments=BANDS * pixels).reshape(
        BANDS, pixels
    )
    weighted = jax.ops.segment_sum(inv_var * mags, segment, num_segments=BANDS * pixels).reshape(
        BANDS, pixels
    )
    local_rhs = jnp.dot(weighted, basis, precision=lax.Precision.HIGHEST)
    root_total = jnp.sqrt(jnp.float32(total_pix))

    def reduce_full(vector):
        return nested_sum(vector, (("tile_0", "tile_1"), ("grp_0", "grp_1")))

    right_side = reduce_full(local_rhs) / root_total
    solution = jnp.zeros_like(right_side)
    residual = right_side
    direction = right_side
    norm_now = jnp.sum(residual * residual)
    for step in range(ITERS):
        model_val = lax.dot_general(
            direction, basis, (((1,), (1,)), ((), ())), precision=lax.Precision.HIGHEST
        )
        scaled = counts * model_val
        image = (
            reduce_full(jnp.dot(scaled, basis, precision=lax.Precision.HIGHEST))
            / jnp.float32(total_pix)
            + ridge * direction
        )
        step_len = norm_now / jnp.sum(direction * image)
        solution = solution + step_len * direction
        residual = residual - step_len * image
        norm_next = jnp.sum(residual * residual)
        direction = residual + norm_next / norm_now * direction
        norm_now = norm_next
    return (solution, residual)


def solution(mesh):
    torus = Mesh(mesh.devices.reshape(4, 8, 4, 2), ("tile_0", "tile_1", "grp_0", "grp_1"))
    placed = (P(TILE_GRP, None), P(TILE_GRP), P(TILE_GRP), P(TILE_GRP), P(TILE_GRP))
    return jax.shard_map(body, mesh=torus, in_specs=placed, out_specs=(P(), P()), check_vma=False)
```

profile of v0, /device:TPU:1, one launch (start us, length us, event | category | flops | bytes accessed | tf_op | source)
XLA Modules:
  0.0 327.6 jit_solution(13577873034647604086)
XLA Ops:
  0.6 0.8 multiply_add_fusion.4
  1.4 0.8 mul.144
  2.2 43.2 %scatter_custom_fusion = f32[2560]{0:T(1024)S(1)} fusion(s32[8192]{0:T(1024)S(1)} %multiply_add_fusion.4, f32[8192]{0:T(1024)S(1)} %mul.144, f32[]{:T(128)} %constant.6.clone.1), kind=kCustom, calls=%fused_computation.28 | custom fusion | flops 8192 | bytes 10244 | tf_op jit(solution)/shard_map/scatter-add | solution.py:73
  45.4 6.4 %fusion.9 = f32[5,2401]{1,0:T(8,128)S(1)} fusion(f32[5,512]{1,0:T(8,128)S(1)} %reshape.83, f32[512,2401]{0,1:T(8,128)} %param.5), kind=kOutput, calls=%fused_computation.33 | convolution fusion | flops 73758720 | bytes 4975508 | tf_op jit(solution)/shard_map/dot_general | solution.py:76
  52.0 0.2 reshape_reshape.24
  52.2 0.2 reshape.111
  52.4 10.4 %all_to_all.100 = f32[8,1,1504]{2,1,0:T(1,128)S(1)} all-to-all(f32[8,1,1504]{2,1,0:T(1,128)S(1)} %reshape.111), channel_id=1, replica_groups=mesh['tile_0'=4,'tile_1'=8,'grp_0'=4,'grp_1'=2] {'grp_0','grp_1'}, dimensions={0} | all-to-all | bytes 96256 | tf_op jit(solution)/shard_map/all_to_all | solution.py:49
  62.8 0.5 broadcast.126
  63.3 0.8 reduce.10
  64.1 0.2 reshape.112
  64.3 19.7 %all_to_all.101 = f32[32,1,47]{2,1,0:T(1,128)S(1)} all-to-all(f32[32,1,47]{2,1,0:T(1,128)S(1)} %bitcast.37), channel_id=1, replica_groups=mesh['tile_0'=4,'tile_1'=8,'grp_0'=4,'grp_1'=2] {'tile_0','tile_1'}, dimensions={0} | all-to-all | bytes 12032 | tf_op jit(solution)/shard_map/all_to_all | solution.py:56
  84.0 11.6 %all_to_all.102 = f32[32,1,47]{2,1,0:T(1,128)S(1)} all-to-all(f32[32,1,47]{2,1,0:T(1,128)S(1)} %broadcast_in_dim.27), channel_id=1, replica_groups=mesh['tile_0'=4,'tile_1'=8,'grp_0'=4,'grp_1'=2] {'tile_0','tile_1'}, dimensions={0} | all-to-all | bytes 12032 | tf_op jit(solution)/shard_map/all_to_all | solution.py:24
  95.7 0.8 reshape.113
  96.5 6.6 %all-to-all-start.3 = ((f32[8,1,1504]{2,1,0:T(1,128)}), f32[8,1,1504]{2,1,0:T(1,128)S(1)}, u32[]{:S(2)}, u32[]{:S(2)}) async-start(f32[8,1,1504]{2,1,0:T(1,128)} %reshape.113), calls=%async_computation.3 | async-start | bytes 98304 | tf_op jit(solution)/shard_map/all_to_all | solution.py:24
  103.1 43.6 %scatter_custom_fusion.1 = f32[2560]{0:T(1024)S(1)} fusion(s32[8192]{0:T(1024)S(1)} %multiply_add_fusion.4, f32[8192]{0:T(1024)} %param.9, f32[]{:T(128)} %constant.6.clone.1), kind=kCustom, calls=%fused_computation.26 | custom fusion | flops 8192 | bytes 10752 | tf_op jit(solution)/shard_map/scatter-add | solution.py:70
  146.7 0.8 reduce.11
  147.5 0.2 reshape.114
  147.8 0.2 reshape_reshape.25
  148.1 5.0 %convolution_multiply_fusion.2 = f32[5,512]{1,0:T(8,128)S(1)} fusion(f32[5,512]{1,0:T(8,128)S(1)} %reshape.85, f32[5,2401]{1,0:T(8,128)S(1)} %div.38, f32[512,2401]{0,1:T(8,128)} %param.5), kind=kOutput, calls=%fused_computation.4 | convolution fusion | flops 73761280 | bytes 4985748 | tf_op jit(solution)/shard_map/dot_general | solution.py:88
  153.1 4.1 %fusion.10 = f32[5,2401]{1,0:T(8,128)S(1)} fusion(f32[5,512]{1,0:T(8,128)S(1)} %convolution_multiply_fusion.2, f32[512,2401]{0,1:T(8,128)S(1)} %copy-done), kind=kOutput, calls=%fused_computation.34 | convolution fusion | flops 73758720 | bytes 4975508 | tf_op jit(solution)/shard_map/dot_general | solution.py:93
  157.3 0.2 reshape_reshape.26
  157.6 0.2 reshape.115
  157.8 9.4 %all_to_all.103 = f32[8,1,1504]{2,1,0:T(1,128)S(1)} all-to-all(f32[8,1,1504]{2,1,0:T(1,128)S(1)} %reshape.115), channel_id=1, replica_groups=mesh['tile_0'=4,'tile_1'=8,'grp_0'=4,'grp_1'=2] {'grp_0','grp_1'}, dimensions={0} | all-to-all | bytes 96256 | tf_op jit(solution)/shard_map/all_to_all | solution.py:49
  167.2 0.8 reduce.12
  168.0 0.2 reshape.116
  168.2 11.6 %all_to_all.104 = f32[32,1,47]{2,1,0:T(1,128)S(1)} all-to-all(f32[32,1,47]{2,1,0:T(1,128)S(1)} %bitcast.39), channel_id=1, replica_groups=mesh['tile_0'=4,'tile_1'=8,'grp_0'=4,'grp_1'=2] {'tile_0','tile_1'}, dimensions={0} | all-to-all | bytes 12032 | tf_op jit(solution)/shard_map/all_to_all | solution.py:56
  179.9 11.6 %all_to_all.105 = f32[32,1,47]{2,1,0:T(1,128)S(1)} all-to-all(f32[32,1,47]{2,1,0:T(1,128)S(1)} %broadcast_in_dim.30), channel_id=1, replica_groups=mesh['tile_0'=4,'tile_1'=8,'grp_0'=4,'grp_1'=2] {'tile_0','tile_1'}, dimensions={0} | all-to-all | bytes 12032 | tf_op jit(solution)/shard_map/all_to_all | solution.py:24
  191.5 0.2 reshape.117
  191.8 10.2 %all_to_all.106 = f32[8,1,1504]{2,1,0:T(1,128)S(1)} all-to-all(f32[8,1,1504]{2,1,0:T(1,128)S(1)} %reshape.117), channel_id=1, replica_groups=mesh['tile_0'=4,'tile_1'=8,'grp_0'=4,'grp_1'=2] {'grp_0','grp_1'}, dimensions={0} | all-to-all | bytes 96256 | tf_op jit(solution)/shard_map/all_to_all | solution.py:24
  202.0 0.8 reduce.13
  202.7 0.2 reshape.118
  203.0 0.2 reshape_reshape.27
  203.2 0.7 multiply_reduce_fusion.4
  205.3 0.6 multiply_reduce_fusion.3
  207.5 4.8 %convolution_multiply_fusion.1 = f32[5,512]{1,0:T(8,128)S(1)} fusion(f32[5,512]{1,0:T(8,128)S(1)} %reshape.85, f32[5,2401]{1,0:T(8,128)S(1)} %get-tuple-element.6, f32[512,2401]{0,1:T(8,128)} %param.5), kind=kOutput, calls=%fused_computation.3 | convolution fusion | flops 73761280 | bytes 4985748 | tf_op jit(solution)/shard_map/dot_general | solution.py:88
  212.3 6.4 %fusion.11 = f32[5,2401]{1,0:T(8,128)S(1)} fusion(f32[5,512]{1,0:T(8,128)S(1)} %convolution_multiply_fusion.1, f32[512,2401]{0,1:T(8,128)} %param.5), kind=kOutput, calls=%fused_computation.35 | convolution fusion | flops 73758720 | bytes 4975508 | tf_op jit(solution)/shard_map/dot_general | solution.py:93
  218.9 0.2 reshape_reshape.28
  219.2 0.2 reshape.119
  219.4 7.9 %all_to_all.107 = f32[8,1,1504]{2,1,0:T(1,128)S(1)} all-to-all(f32[8,1,1504]{2,1,0:T(1,128)S(1)} %reshape.119), channel_id=1, replica_groups=mesh['tile_0'=4,'tile_1'=8,'grp_0'=4,'grp_1'=2] {'grp_0','grp_1'}, dimensions={0} | all-to-all | bytes 96256 | tf_op jit(solution)/shard_map/all_to_all | solution.py:49
  227.3 0.8 reduce.14
  228.0 0.2 reshape.120
  228.3 11.6 %all_to_all.108 = f32[32,1,47]{2,1,0:T(1,128)S(1)} all-to-all(f32[32,1,47]{2,1,0:T(1,128)S(1)} %bitcast.41), channel_id=1, replica_groups=mesh['tile_0'=4,'tile_1'=8,'grp_0'=4,'grp_1'=2] {'tile_0','tile_1'}, dimensions={0} | all-to-all | bytes 12032 | tf_op jit(solution)/shard_map/all_to_all | solution.py:56
  240.0 11.6 %all_to_all.109 = f32[32,1,47]{2,1,0:T(1,128)S(1)} all-to-all(f32[32,1,47]{2,1,0:T(1,128)S(1)} %broadcast_in_dim.33), channel_id=1, replica_groups=mesh['tile_0'=4,'tile_1'=8,'grp_0'=4,'grp_1'=2] {'tile_0','tile_1'}, dimensions={0} | all-to-all | bytes 12032 | tf_op jit(solution)/shard_map/all_to_all | solution.py:24
  251.6 0.2 reshape.121
  251.8 10.2 %all_to_all.110 = f32[8,1,1504]{2,1,0:T(1,128)S(1)} all-to-all(f32[8,1,1504]{2,1,0:T(1,128)S(1)} %reshape.121), channel_id=1, replica_groups=mesh['tile_0'=4,'tile_1'=8,'grp_0'=4,'grp_1'=2] {'grp_0','grp_1'}, dimensions={0} | all-to-all | bytes 96256 | tf_op jit(solution)/shard_map/all_to_all | solution.py:24
  262.0 0.8 reduce.15
  263.1 0.2 reshape_reshape.29
  263.3 0.7 multiply_reduce_fusion.2
  265.4 0.7 multiply_reduce_fusion.1
  267.5 4.8 %convolution_multiply_fusion = f32[5,512]{1,0:T(8,128)S(1)} fusion(f32[5,512]{1,0:T(8,128)S(1)} %reshape.85, f32[512,2401]{0,1:T(8,128)} %param.5, f32[5,2401]{1,0:T(8,128)S(1)} %get-tuple-element.6, f32[]{:T(128)S(6)} %div.44, f32[5,2401]{1,0:T(8,128)S(1)} %get-tuple-element.7, f32[5,2401]{1,0:T(8,128)S(1)} %div.45, f32[]{:T(128)S(6)} %div.43), kind=kOutput, calls=%fused_computation.2 | convolution fusion | flops 73833312 | bytes 5081796 | tf_op jit(solution)/shard_map/dot_general | solution.py:88
  272.4 6.4 %fusion.12 = f32[5,2401]{1,0:T(8,128)S(1)} fusion(f32[5,512]{1,0:T(8,128)S(1)} %convolution_multiply_fusion, f32[512,2401]{0,1:T(8,128)} %param.5), kind=kOutput, calls=%fused_computation.36 | convolution fusion | flops 73758720 | bytes 4975508 | tf_op jit(solution)/shard_map/dot_general | solution.py:93
  278.9 0.2 reshape_reshape.30
  279.2 0.2 reshape.123
  279.4 7.9 %all_to_all.111 = f32[8,1,1504]{2,1,0:T(1,128)S(1)} all-to-all(f32[8,1,1504]{2,1,0:T(1,128)S(1)} %reshape.123), channel_id=1, replica_groups=mesh['tile_0'=4,'tile_1'=8,'grp_0'=4,'grp_1'=2] {'grp_0','grp_1'}, dimensions={0} | all-to-all | bytes 96256 | tf_op jit(solution)/shard_map/all_to_all | solution.py:49
  287.3 0.8 reduce.16
  288.3 11.6 %all_to_all.112 = f32[32,1,47]{2,1,0:T(1,128)S(1)} all-to-all(f32[32,1,47]{2,1,0:T(1,128)S(1)} %bitcast.43), channel_id=1, replica_groups=mesh['tile_0'=4,'tile_1'=8,'grp_0'=4,'grp_1'=2] {'tile_0','tile_1'}, dimensions={0} | all-to-all | bytes 12032 | tf_op jit(solution)/shard_map/all_to_all | solution.py:56
  300.0 11.6 %all_to_all.113 = f32[32,1,47]{2,1,0:T(1,128)S(1)} all-to-all(f32[32,1,47]{2,1,0:T(1,128)S(1)} %broadcast_in_dim.70), channel_id=1, replica_groups=mesh['tile_0'=4,'tile_1'=8,'grp_0'=4,'grp_1'=2] {'tile_0','tile_1'}, dimensions={0} | all-to-all | bytes 12032 | tf_op jit(solution)/shard_map/all_to_all | solution.py:24
  311.6 0.8 reshape.125
  312.5 6.3 %all-to-all-start.15 = ((f32[8,1,1504]{2,1,0:T(1,128)}), f32[8,1,1504]{2,1,0:T(1,128)S(1)}, u32[]{:S(2)}, u32[]{:S(2)}) async-start(f32[8,1,1504]{2,1,0:T(1,128)} %reshape.125), calls=%async_computation.15 | async-start | bytes 98304 | tf_op jit(solution)/shard_map/all_to_all | solution.py:24
  318.9 4.7 %all-to-all-done.15 = f32[8,1,1504]{2,1,0:T(1,128)S(1)} async-done(((f32[8,1,1504]{2,1,0:T(1,128)}), f32[8,1,1504]{2,1,0:T(1,128)S(1)}, u32[]{:S(2)}, u32[]{:S(2)}) %all-to-all-start.15) | async-done | bytes 48160 | tf_op jit(solution)/shard_map/all_to_all | solution.py:24
  323.6 0.8 reduce.17
  324.6 0.2 reshape_reshape.31
  324.8 0.6 slice_multiply_fusion
  326.9 0.7 multiply_subtract_fusion
  (49 shorter events, 2.3 us)
Async XLA Ops:
  96.5 50.2 %all-to-all-start.3 = ((f32[8,1,1504]{2,1,0:T(1,128)}), f32[8,1,1504]{2,1,0:T(1,128)S(1)}, u32[]{:S(2)}, u32[]{:S(2)}) async-start(f32[8,1,1504]{2,1,0:T(1,128)} %reshape.113), calls=%async_computation.3 | async-start | bytes 98304 | tf_op jit(solution)/shard_map/all_to_all | solution.py:24
  148.1 5.0 %copy-start = (f32[512,2401]{0,1:T(8,128)S(1)}, f32[512,2401]{0,1:T(8,128)}, u32[]{:S(2)}) copy-start(f32[512,2401]{0,1:T(8,128)} %param.5) | copy-start | bytes 14751748
  312.5 11.1 %all-to-all-start.15 = ((f32[8,1,1504]{2,1,0:T(1,128)}), f32[8,1,1504]{2,1,0:T(1,128)S(1)}, u32[]{:S(2)}, u32[]{:S(2)}) async-start(f32[8,1,1504]{2,1,0:T(1,128)} %reshape.125), calls=%async_computation.15 | async-start | bytes 98304 | tf_op jit(solution)/shard_map/all_to_all | solution.py:24
where the time goes:
time: 329 us; the launch traced here: 328 us
  blocking collectives  157 us (48%)
  other arithmetic  98.8 us (30%)
  matrix products  38.1 us (12%)
  starting transfers between devices  12.9 us (4%)
  between operations  8.05 us (2%)
  local copies, waits for them, and re-layouts  8.01 us (2%)
  waiting for transfers between devices  4.72 us (1%)
    all_to_all x6, blocking collectives, copy_for_each(): lax.all_to_all(jnp.broadcast_to(array[None], (size, *array.shape)), axis,...  66.9 us
    all_to_all x4, blocking collectives, summed_rows(): return jnp.sum(lax.all_to_all(own, far, 0, 0, tiled=True), axis=0)  54.6 us
    scatter-add x1, other arithmetic, body(): jax.ops.segment_sum(inv_var, segment, num_segments=BANDS * pixels)  43.6 us
    scatter-add x1, other arithmetic, body(): jax.ops.segment_sum(inv_var * mags, segment, num_segments=BANDS * pixels)  43.2 us
    all_to_all x4, blocking collectives, sum_at_owner(): parts = lax.all_to_all(split_up(array, dim, size), axis, 0, 0, tiled=True)  35.6 us
    dot_general x3, matrix products, body(): jnp.dot(scaled, basis, precision=lax.Precision.HIGHEST)  17 us
    dot_general x3, matrix products, body(): lax.dot_general(direction, basis, (((1,), (1,)), ((), ())), precision=lax...  14.6 us
    all_to_all x2, starting transfers between devices, copy_for_each(): lax.all_to_all(jnp.broadcast_to(array[None], (size, *array.shape)), axis,...  12.9 us
  transfers between devices with their start and end apart: 2, of which 1 were waited for; matrix products, arithmetic and copies ran while one was open for 13% of the time, Pallas kernels for 0%

commit v1 on v0

v1 whole, which is shorter than its diff:
```python
import functools

import jax
import jax.numpy as jnp
from jax import lax
from jax.experimental import pallas as pl
from jax.experimental.pallas import tpu as pltpu
from jax.sharding import Mesh
from jax.sharding import PartitionSpec as P

BANDS = 5
ITERS = 3
AXES = ("y", "z", "x", "c")
SPAN = {"y": 4, "z": 8, "x": 4, "c": 2}
RIDGE = 0.1
PIX = 512
NCOEF = 2401
LANES = 128
TILES = -(-NCOEF // LANES)
WIDE = TILES * LANES
ROWS = 96
HALF = ROWS // 2
OBJ_ROWS = 64
STRIPES = PIX // LANES
NT = (((1,), (1,)), ((), ()))
NN = (((1,), (0,)), ((), ()))
F32, BF16 = jnp.float32, jnp.bfloat16


def dot(a, b, dims):
    return lax.dot_general(a, b, dims, preferred_element_type=F32)


def split(x):
    high = x.astype(BF16)
    return high, (x - high.astype(F32)).astype(BF16)


def image_of(scaled, high_ref, low_ref, core_ref, full, mine_ref, other_ref):
    both = jnp.concatenate(split(scaled), axis=0)
    total = dot(high_ref[...], both, NT) + dot(low_ref[...], both, NT)
    for j in range(TILES):
        turned = total[j * LANES : (j + 1) * LANES, :].T
        full[j * BANDS : (j + 1) * BANDS, :] = turned[:BANDS] + turned[8 : 8 + BANDS]
    full[TILES * BANDS :, :] = jnp.zeros((ROWS - TILES * BANDS, LANES), F32)
    first = core_ref[0:1, :] == 0
    for out, one, two in ((mine_ref, 0, HALF), (other_ref, HALF, 0)):
        out[...] = jnp.where(first, full[one : one + HALF, :], full[two : two + HALF, :])


def first_kernel(core_ref, basis_hbm, pix_hbm, band_hbm, mag_hbm, var_hbm, mine_ref, other_ref, counts_ref, high_ref, low_ref,
                 raw, pix_ref, band_ref, mag_ref, var_ref, left, right, full, sems, obj_sems):
    obj_copies = [
        pltpu.make_async_copy(src, dst, obj_sems.at[i])
        for i, (src, dst) in enumerate(((pix_hbm, pix_ref), (band_hbm, band_ref), (mag_hbm, mag_ref), (var_hbm, var_ref)))
    ]
    copies = [
        pltpu.make_async_copy(basis_hbm.at[:, pl.ds(i * LANES, LANES)], raw.at[:, pl.ds(i * LANES, LANES)], sems.at[i])
        for i in range(STRIPES)
    ]
    for copy in obj_copies + copies:
        copy.start()
    group_no = lax.broadcasted_iota(jnp.int32, (32, LANES), 0)
    lane_no = lax.broadcasted_iota(jnp.int32, (LANES, LANES), 0)

    for copy in obj_copies:
        copy.wait()

    def objects(block, carry):
        at = pl.multiple_of(block * 8, 8)
        pix = pix_ref[pl.ds(at, 8), :]
        band = band_ref[pl.ds(at, 8), :]
        var = var_ref[pl.ds(at, 8), :]
        weight = var * mag_ref[pl.ds(at, 8), :]
        group = lax.shift_right_logical(pix, 7) * 8 + band
        low_pix = lax.bitwise_and(pix, LANES - 1)
        values = []
        for v in (var, weight):
            high = v.astype(BF16).astype(F32)
            values += [high, v - high]
        for i in range(8):
            mine = group_no == group[i : i + 1, :]
            to = pl.ds(pl.multiple_of(block * 8 * LANES, 8 * LANES) + i * LANES, LANES)
            for k, v in enumerate(values):
                left[k * 32 : (k + 1) * 32, to] = jnp.where(mine, v[i : i + 1, :], 0.0).astype(BF16)
            right[:, to] = jnp.where(lane_no == low_pix[i : i + 1, :], 1.0, 0.0).astype(BF16)
        return carry

    lax.fori_loop(0, OBJ_ROWS // 8, objects, 0)
    sums = dot(left[...], right[...], NT)
    counts, weighted = [
        jnp.concatenate([sums[q + h * 8 : q + h * 8 + 8] + sums[q + 32 + h * 8 : q + 40 + h * 8] for h in range(4)], axis=1)
        for q in (0, 64)
    ]
    counts_ref[...] = counts
    edge = NCOEF // 16 * 16
    for i, copy in enumerate(copies):
        copy.wait()
        cols = pl.ds(i * LANES, LANES)
        for row in range(0, edge, 160):
            rows = pl.ds(row, 160)
            high_ref[rows, cols], low_ref[rows, cols] = split(raw[rows, cols])
        tail = jnp.broadcast_to(raw[edge:NCOEF, cols], (WIDE - edge, LANES))
        tail = jnp.where(lax.broadcasted_iota(jnp.int32, tail.shape, 0) == 0, tail, 0.0)
        high_ref[edge:, cols], low_ref[edge:, cols] = split(tail)
    image_of(weighted, high_ref, low_ref, core_ref, full, mine_ref, other_ref)


def model_and_image(direction, wide, counts_ref, high_ref, low_ref, core_ref, full, mine_ref, other_ref):
    wide[...] = jnp.zeros_like(wide)
    for j in range(TILES):
        wide[:BANDS, j * LANES : (j + 1) * LANES] = direction[j * BANDS : (j + 1) * BANDS, :]
    both = jnp.concatenate(split(wide[...]), axis=0)
    model = dot(both, high_ref[...], NN) + dot(both, low_ref[...], NN)
    image_of(counts_ref[...] * (model[:8] + model[8:]), high_ref, low_ref, core_ref, full, mine_ref, other_ref)


def joined(core_ref, own_ref, near_ref):
    first = core_ref[0:1, :] == 0
    own, near = own_ref[...], near_ref[...]
    return jnp.concatenate([jnp.where(first, own, near), jnp.where(first, near, own)], axis=0)


def total_of(x):
    return jnp.sum(x, keepdims=True)


def start_kernel(root, core_ref, own, near, counts_ref, high_ref, low_ref,
                 mine_ref, other_ref, res_ref, norm_ref, wide, full):
    right_side = joined(core_ref, own, near) / root
    res_ref[...] = right_side
    norm_ref[...] = jnp.broadcast_to(total_of(right_side * right_side), (8, LANES))
    model_and_image(right_side, wide, counts_ref, high_ref, low_ref, core_ref, full, mine_ref, other_ref)


def advance(pixels, whole, sol, res, direction, norm):
    image = whole / pixels + RIDGE * direction
    step = norm / total_of(direction * image)
    sol = sol + step * direction
    res = res - step * image
    norm_next = total_of(res * res)
    return sol, res, res + norm_next / norm * direction, norm_next


def step_kernel(pixels, core_ref, own, near, sol_ref, res_ref, dir_ref, norm_ref, counts_ref, high_ref, low_ref,
                mine_ref, other_ref, sol_out, res_out, dir_out, norm_out, wide, full):
    sol, res, direction, norm = advance(
        pixels, joined(core_ref, own, near), sol_ref[...], res_ref[...], dir_ref[...], norm_ref[0:1, 0:1]
    )
    sol_out[...] = sol
    res_out[...] = res
    dir_out[...] = direction
    norm_out[...] = jnp.broadcast_to(norm, (8, LANES))
    model_and_image(direction, wide, counts_ref, high_ref, low_ref, core_ref, full, mine_ref, other_ref)


def last_kernel(pixels, core_ref, own, near, sol_ref, res_ref, dir_ref, norm_ref, sol_out, res_out):
    sol, res, _, _ = advance(
        pixels, joined(core_ref, own, near), sol_ref[...], res_ref[...], dir_ref[...], norm_ref[0:1, 0:1]
    )
    for value, out in ((sol, sol_out), (res, res_out)):
        for j in range(TILES):
            width = min(LANES, NCOEF - j * LANES)
            out[:, j * LANES : j * LANES + width] = value[j * BANDS : (j + 1) * BANDS, :width]


VMEM = pl.BlockSpec(memory_space=pltpu.VMEM)
HBM = pl.BlockSpec(memory_space=pltpu.HBM)
LIMIT = 24 * 1024 * 1024


def shape(*dims, kind=F32):
    return jax.ShapeDtypeStruct(dims, kind)


def call(kernel, name, outs, ins, scratch=(), limit=LIMIT):
    return pl.pallas_call(
        kernel,
        name=name,
        out_shape=outs,
        in_specs=ins,
        out_specs=[VMEM] * len(outs),
        scratch_shapes=list(scratch),
        compiler_params=pltpu.CompilerParams(vmem_limit_bytes=limit),
    )


def sum_up(parts):
    total = parts[0]
    for i in range(1, parts.shape[0]):
        total = total + parts[i]
    return total


def device(y, z, x, c):
    return ((y * SPAN["z"] + z) * SPAN["x"] + x) * SPAN["c"] + c


def two_rounds():
    ys, zs, xs, pairs = range(SPAN["y"]), range(SPAN["z"]), range(SPAN["x"]), range(SPAN["y"] // 2)
    spread = sorted(zs, key=lambda z: (z % 2, z // 2 % 2, z))
    one = [[device(y, z, x, 0) for y in ys for x in xs] for z in zs]
    one += [[device(2 * pair + k, z, x, 1) for z in zs for k in (0, 1)] for x in xs for pair in pairs]
    two = [[device(y, z, x, 0) for z in spread] for y in ys for x in xs]
    two += [[device(y, z, x, 1) for x in xs for y in take] for z in zs for take in ((0, 3), (1, 2))]
    return one, two


def sent_to_all(block, groups):
    size = len(groups[0])
    sent = jnp.broadcast_to(block[None], (size, *block.shape))
    return sum_up(lax.all_to_all(sent, AXES, 0, 0, tiled=True, axis_index_groups=groups))


def summed(mine, other):
    swap = [(0, 1), (1, 0)]
    mine = mine + lax.ppermute(other, "c", swap)
    for groups in two_rounds():
        mine = sent_to_all(mine, groups)
    return mine, lax.ppermute(mine, "c", swap)


def body(basis, pixel_ids, band_ids, mags, inv_var):
    pixels = float(PIX * 256)
    objects = [a.reshape(OBJ_ROWS, LANES) for a in (pixel_ids, band_ids, mags, inv_var)]
    core = jnp.broadcast_to(lax.axis_index("c"), (8, LANES)).astype(jnp.int32)
    vec, half, norm_shape = shape(ROWS, LANES), shape(HALF, LANES), shape(8, LANES)
    scratch = [pltpu.VMEM((8, WIDE), F32), pltpu.VMEM((ROWS, LANES), F32)]
    copied = shape(WIDE, PIX, kind=BF16)
    mine, other, counts, high, low = call(
        first_kernel,
        "first",
        [half, half, shape(8, PIX), copied, copied],
        [VMEM] + [HBM] * 5,
        [
            pltpu.VMEM((NCOEF, PIX), F32),
            pltpu.VMEM((OBJ_ROWS, LANES), jnp.int32),
            pltpu.VMEM((OBJ_ROWS, LANES), jnp.int32),
            pltpu.VMEM((OBJ_ROWS, LANES), F32),
            pltpu.VMEM((OBJ_ROWS, LANES), F32),
            pltpu.VMEM((128, OBJ_ROWS * LANES), BF16),
            pltpu.VMEM((128, OBJ_ROWS * LANES), BF16),
            pltpu.VMEM((ROWS, LANES), F32),
            pltpu.SemaphoreType.DMA((STRIPES,)),
            pltpu.SemaphoreType.DMA((4,)),
        ],
    )(core, *[pltpu.with_memory_space_constraint(a, pltpu.HBM) for a in (basis.T, *objects)])
    mine, other, res, norm = call(
        functools.partial(start_kernel, pixels**0.5), "start", [half, half, vec, norm_shape], [VMEM] * 6, scratch
    )(core, *summed(mine, other), counts, high, low)
    sol, direction = jnp.zeros((ROWS, LANES), F32), res
    for _ in range(ITERS - 1):
        mine, other, sol, res, direction, norm = call(
            functools.partial(step_kernel, pixels), "step", [half, half, vec, vec, vec, norm_shape], [VMEM] * 10, scratch
        )(core, *summed(mine, other), sol, res, direction, norm, counts, high, low)
    out = shape(BANDS, NCOEF)
    return tuple(
        call(functools.partial(last_kernel, pixels), "last", [out, out], [VMEM] * 7)(
            core, *summed(mine, other), sol, res, direction, norm
        )
    )


def solution(mesh):
    torus = Mesh(mesh.devices.reshape(*(SPAN[a] for a in AXES)), AXES)
    return jax.shard_map(
        body,
        mesh=torus,
        in_specs=(P(AXES, None),) + (P(AXES),) * 4,
        out_specs=(P(), P()),
        check_vma=False,
    )
```

time: 329 us -> 137 us (0.42)
  other arithmetic: 98.8 us -> 0.19 us
  blocking collectives: 157 us -> 103 us
  matrix products: 38.1 us -> 0 us
  Pallas kernels: 0 us -> 15.8 us
  local copies, waits for them, and re-layouts: 8.01 us -> 0.18 us
  between operations: 8.05 us -> 0.73 us
    scatter-add x2 -> x0, other arithmetic: 86.8 us -> none  [the longest x1 43.6 us: body(): jax.ops.segment_sum(inv_var, segment, num_segments=BANDS * pixels)]
    all_to_all x14 -> x8, blocking collectives: 157 us -> 103 us  [sent_to_all(): lax.all_to_all(sent, AXES, 0, 0, tiled=True, axis_index_groups=groups)]
    dot_general x7 -> x0, matrix products: 38.1 us -> none  [the longest x3 17 us: body(): jnp.dot(scaled, basis, precision=lax.Precision.HIGHEST)]
    pallas_call x0 -> x5, Pallas kernels: none -> 15.8 us  [the longest x1 7.6 us: body(): call(first_kernel, 'first', [half, half, shape(8, PIX), copied, copied],...]
    all_to_all x2 -> x0, starting transfers between devices: 12.9 us -> none  [copy_for_each(): lax.all_to_all(jnp.broadcast_to(array[None], (size, *array.shape)), axis,...]
    ppermute x0 -> x8, starting transfers between devices: none -> 10.1 us  [the longest x4 5.61 us: summed(): return (mine, lax.ppermute(mine, 'c', swap))]
    ppermute x0 -> x8, waiting for transfers between devices: none -> 6.8 us  [the longest x4 3.4 us: summed(): mine = mine + lax.ppermute(other, 'c', swap)]
    all_to_all x8 -> x0, other arithmetic: 6.09 us -> none  [the longest x4 3.05 us: copy_for_each(): lax.all_to_all(jnp.broadcast_to(array[None], (size, *array.shape)), axis,...]
  transfers between devices with their start and end apart: 2 -> 8, of which waited for: 1 -> 8; matrix products, arithmetic and copies ran while one was open for 13% -> 0% of each run, Pallas kernels for 0% -> 0%
where the time goes in v1:
time: 137 us
  blocking collectives  103 us (75%)
  Pallas kernels  15.8 us (12%)
  starting transfers between devices  10.1 us (7%)
  waiting for transfers between devices  6.8 us (5%)
    all_to_all x8, blocking collectives, sent_to_all(): lax.all_to_all(sent, AXES, 0, 0, tiled=True, axis_index_groups=groups)  103 us
    pallas_call x1, Pallas kernels, body(): call(first_kernel, 'first', [half, half, shape(8, PIX), copied, copied],...  7.6 us
    ppermute x4, starting transfers between devices, summed(): return (mine, lax.ppermute(mine, 'c', swap))  5.61 us
    pallas_call x2, Pallas kernels, body(): call(functools.partial(step_kernel, pixels), 'step', [half, half, vec, ve...  5.12 us
    ppermute x4, starting transfers between devices, summed(): mine = mine + lax.ppermute(other, 'c', swap)  4.52 us
    ppermute x4, waiting for transfers between devices, summed(): mine = mine + lax.ppermute(other, 'c', swap)  3.4 us
    ppermute x4, waiting for transfers between devices, summed(): return (mine, lax.ppermute(mine, 'c', swap))  3.4 us
  transfers between devices with their start and end apart: 8, of which 8 were waited for; matrix products, arithmetic and copies ran while one was open for 0% of the time, Pallas kernels for 0%

profile of v1, /device:TPU:1, one launch (start us, length us, event | category | flops | bytes accessed | tf_op | source)
XLA Modules:
  0.0 136.6 jit_solution(11210601689408153206)
XLA Ops:
  0.6 7.6 %first.1 = (f32[48,128]{1,0:T(8,128)S(1)}, f32[48,128]{1,0:T(8,128)S(1)}, f32[8,512]{1,0:T(8,128)S(1)}, bf16[2432,512]{1,0:T(8,128)(2,1)S(1)}, bf16[2432,512]{1,0:T(8,128)(2,1)S(1)}) custom-call(s32[8,128]{1,0:T(8,128)S(1)} %broadcast_in_dim.28.core_ref, f32[2401,512]{1,0:T(8,128)} %bitcast.21, s32[64,128]{1,0:T(8,128)} %bitcast.22, s32[64,128]{1,0:T(8,128)} %bitcast.23, ...), custom_call_target="tpu_custom_call" | custom-call | tf_op jit(solution)/shard_map/first/pallas_call | solution.py:230
  8.2 3.3 %collective-permute-start = (f32[48,128]{1,0:T(8,128)S(1)}, f32[48,128]{1,0:T(8,128)S(1)}, u32[]{:S(2)}, u32[]{:S(2)}) collective-permute-start(f32[48,128]{1,0:T(8,128)S(1)} %get-tuple-element.24), channel_id=1, source_target_pairs={{0,1},{1,0},{2,3},{3,2},{4,5},{5,4},{6,7},{7,6},{8,9},{9,8},{10,11... | collective-permute-start | bytes 73736 | tf_op jit(solution)/shard_map/ppermute | solution.py:217
  11.5 0.8 collective-permute-done
  12.4 18.1 %all_to_all.40 = f32[16,48,128]{2,1,0:T(8,128)S(1)} all-to-all(f32[16,48,128]{2,1,0:T(8,128)S(1)} %broadcast_in_dim.29), channel_id=1, replica_groups={{0,2,4,6,64,66,68,70,128,130,132,134,192,194,196,198},{8,10,12,14,72,74..., dimensions={0} | all-to-all | bytes 786432 | tf_op jit(solution)/shard_map/all_to_all | solution.py:212
  30.6 12.0 %all_to_all.41 = f32[8,48,128]{2,1,0:T(8,128)S(1)} all-to-all(f32[8,48,128]{2,1,0:T(8,128)S(1)} %broadcast_in_dim.31), channel_id=1, replica_groups={{0,32,16,48,8,40,24,56},{2,34,18,50,10,42,26,58},{4,36,20,52,12,44,28,6..., dimensions={0} | all-to-all | bytes 393216 | tf_op jit(solution)/shard_map/all_to_all | solution.py:212
  42.6 1.2 collective-permute-start.1
  43.8 0.8 collective-permute-done.1.near
  44.6 2.2 %start.1 = (f32[48,128]{1,0:T(8,128)S(1)}, f32[48,128]{1,0:T(8,128)S(1)}, f32[96,128]{1,0:T(8,128)S(1)}, f32[8,128]{1,0:T(8,128)S(1)}) custom-call(s32[8,128]{1,0:T(8,128)S(1)} %broadcast_in_dim.28.core_ref, f32[48,128]{1,0:T(8,128)S(1)} %fusion.6.own, f32[48,128]{1,0:T(8,128)S(1)} %collective-permute-done.1.near, ...), custom_call_target="tpu_custom_call" | custom-call | tf_op jit(solution)/shard_map/start/pallas_call | solution.py:248
  46.9 0.4 collective-permute-start.2
  47.3 0.8 collective-permute-done.2
  48.2 14.0 %all_to_all.42 = f32[16,48,128]{2,1,0:T(8,128)S(1)} all-to-all(f32[16,48,128]{2,1,0:T(8,128)S(1)} %broadcast_in_dim.32), channel_id=1, replica_groups={{0,2,4,6,64,66,68,70,128,130,132,134,192,194,196,198},{8,10,12,14,72,74..., dimensions={0} | all-to-all | bytes 786432 | tf_op jit(solution)/shard_map/all_to_all | solution.py:212
  62.3 10.1 %all_to_all.43 = f32[8,48,128]{2,1,0:T(8,128)S(1)} all-to-all(f32[8,48,128]{2,1,0:T(8,128)S(1)} %broadcast_in_dim.68), channel_id=1, replica_groups={{0,32,16,48,8,40,24,56},{2,34,18,50,10,42,26,58},{4,36,20,52,12,44,28,6..., dimensions={0} | all-to-all | bytes 393216 | tf_op jit(solution)/shard_map/all_to_all | solution.py:212
  72.4 1.4 %collective-permute-start.3 = (f32[48,128]{1,0:T(8,128)S(1)}, f32[48,128]{1,0:T(8,128)S(1)}, u32[]{:S(2)}, u32[]{:S(2)}) collective-permute-start(f32[48,128]{1,0:T(8,128)S(1)} %fusion.4.own), channel_id=1, source_target_pairs={{0,1},{1,0},{2,3},{3,2},{4,5},{5,4},{6,7},{7,6},{8,9},{9,8},{10,11... | collective-permute-start | bytes 73736 | tf_op jit(solution)/shard_map/ppermute | solution.py:220
  73.8 0.8 collective-permute-done.3.near
  74.7 2.6 %step.2 = (f32[48,128]{1,0:T(8,128)S(1)}, f32[48,128]{1,0:T(8,128)S(1)}, f32[96,128]{1,0:T(8,128)S(1)}, f32[96,128]{1,0:T(8,128)S(1)}, f32[96,128]{1,0:T(8,128)S(1)}, /*index=5*/f32[8,128]{1,0:T(8,128)S(1)}) custom-call(s32[8,128]{1,0:T(8,128)S(1)} %broadcast_in_dim.28.core_ref, f32[48,128]{1,0:T(8,128)S(1)} %fusion.4.own, ...), custom_call_target="tpu_custom_call" | custom-call | tf_op jit(solution)/shard_map/step/pallas_call | solution.py:253
  77.2 0.4 collective-permute-start.4
  77.6 0.8 collective-permute-done.4
  78.5 14.0 %all_to_all.44 = f32[16,48,128]{2,1,0:T(8,128)S(1)} all-to-all(f32[16,48,128]{2,1,0:T(8,128)S(1)} %broadcast_in_dim.70), channel_id=1, replica_groups={{0,2,4,6,64,66,68,70,128,130,132,134,192,194,196,198},{8,10,12,14,72,74..., dimensions={0} | all-to-all | bytes 786432 | tf_op jit(solution)/shard_map/all_to_all | solution.py:212
  92.6 10.2 %all_to_all.45 = f32[8,48,128]{2,1,0:T(8,128)S(1)} all-to-all(f32[8,48,128]{2,1,0:T(8,128)S(1)} %broadcast_in_dim.72), channel_id=1, replica_groups={{0,32,16,48,8,40,24,56},{2,34,18,50,10,42,26,58},{4,36,20,52,12,44,28,6..., dimensions={0} | all-to-all | bytes 393216 | tf_op jit(solution)/shard_map/all_to_all | solution.py:212
  102.8 1.6 %collective-permute-start.5 = (f32[48,128]{1,0:T(8,128)S(1)}, f32[48,128]{1,0:T(8,128)S(1)}, u32[]{:S(2)}, u32[]{:S(2)}) collective-permute-start(f32[48,128]{1,0:T(8,128)S(1)} %fusion.2.own), channel_id=1, source_target_pairs={{0,1},{1,0},{2,3},{3,2},{4,5},{5,4},{6,7},{7,6},{8,9},{9,8},{10,11... | collective-permute-start | bytes 73736 | tf_op jit(solution)/shard_map/ppermute | solution.py:220
  104.4 0.8 collective-permute-done.5.near
  105.3 2.6 %step.3 = (f32[48,128]{1,0:T(8,128)S(1)}, f32[48,128]{1,0:T(8,128)S(1)}, f32[96,128]{1,0:T(8,128)S(1)}, f32[96,128]{1,0:T(8,128)S(1)}, f32[96,128]{1,0:T(8,128)S(1)}, /*index=5*/f32[8,128]{1,0:T(8,128)S(1)}) custom-call(s32[8,128]{1,0:T(8,128)S(1)} %broadcast_in_dim.28.core_ref, f32[48,128]{1,0:T(8,128)S(1)} %fusion.2.own, ...), custom_call_target="tpu_custom_call" | custom-call | tf_op jit(solution)/shard_map/step/pallas_call | solution.py:253
  107.9 0.4 collective-permute-start.6
  108.3 0.8 collective-permute-done.6
  109.2 14.1 %all_to_all.46 = f32[16,48,128]{2,1,0:T(8,128)S(1)} all-to-all(f32[16,48,128]{2,1,0:T(8,128)S(1)} %broadcast_in_dim.73), channel_id=1, replica_groups={{0,2,4,6,64,66,68,70,128,130,132,134,192,194,196,198},{8,10,12,14,72,74..., dimensions={0} | all-to-all | bytes 786432 | tf_op jit(solution)/shard_map/all_to_all | solution.py:212
  123.3 10.2 %all_to_all.47 = f32[8,48,128]{2,1,0:T(8,128)S(1)} all-to-all(f32[8,48,128]{2,1,0:T(8,128)S(1)} %broadcast_in_dim.75), channel_id=1, replica_groups={{0,32,16,48,8,40,24,56},{2,34,18,50,10,42,26,58},{4,36,20,52,12,44,28,6..., dimensions={0} | all-to-all | bytes 393216 | tf_op jit(solution)/shard_map/all_to_all | solution.py:212
  133.5 1.4 %collective-permute-start.7 = (f32[48,128]{1,0:T(8,128)S(1)}, f32[48,128]{1,0:T(8,128)S(1)}, u32[]{:S(2)}, u32[]{:S(2)}) collective-permute-start(f32[48,128]{1,0:T(8,128)S(1)} %fusion.own), channel_id=1, source_target_pairs={{0,1},{1,0},{2,3},{3,2},{4,5},{5,4},{6,7},{7,6},{8,9},{9,8},{10,11... | collective-permute-start | bytes 73736 | tf_op jit(solution)/shard_map/ppermute | solution.py:220
  134.9 0.8 collective-permute-done.7.near
  135.8 0.8 last.1
  (22 shorter events, 0.4 us)
Async XLA Ops:
  8.2 4.1 %collective-permute-start = (f32[48,128]{1,0:T(8,128)S(1)}, f32[48,128]{1,0:T(8,128)S(1)}, u32[]{:S(2)}, u32[]{:S(2)}) collective-permute-start(f32[48,128]{1,0:T(8,128)S(1)} %get-tuple-element.24), channel_id=1, source_target_pairs={{0,1},{1,0},{2,3},{3,2},{4,5},{5,4},{6,7},{7,6},{8,9},{9,8},{10,11... | collective-permute-start | bytes 73736 | tf_op jit(solution)/shard_map/ppermute | solution.py:217
  42.6 2.0 %collective-permute-start.1 = (f32[48,128]{1,0:T(8,128)S(1)}, f32[48,128]{1,0:T(8,128)S(1)}, u32[]{:S(2)}, u32[]{:S(2)}) collective-permute-start(f32[48,128]{1,0:T(8,128)S(1)} %fusion.6.own), channel_id=1, source_target_pairs={{0,1},{1,0},{2,3},{3,2},{4,5},{5,4},{6,7},{7,6},{8,9},{9,8},{10,11... | collective-permute-start | bytes 73736 | tf_op jit(solution)/shard_map/ppermute | solution.py:220
  46.9 1.3 collective-permute-start.2
  72.4 2.2 %collective-permute-start.3 = (f32[48,128]{1,0:T(8,128)S(1)}, f32[48,128]{1,0:T(8,128)S(1)}, u32[]{:S(2)}, u32[]{:S(2)}) collective-permute-start(f32[48,128]{1,0:T(8,128)S(1)} %fusion.4.own), channel_id=1, source_target_pairs={{0,1},{1,0},{2,3},{3,2},{4,5},{5,4},{6,7},{7,6},{8,9},{9,8},{10,11... | collective-permute-start | bytes 73736 | tf_op jit(solution)/shard_map/ppermute | solution.py:220
  77.2 1.3 collective-permute-start.4
  102.8 2.5 %collective-permute-start.5 = (f32[48,128]{1,0:T(8,128)S(1)}, f32[48,128]{1,0:T(8,128)S(1)}, u32[]{:S(2)}, u32[]{:S(2)}) collective-permute-start(f32[48,128]{1,0:T(8,128)S(1)} %fusion.2.own), channel_id=1, source_target_pairs={{0,1},{1,0},{2,3},{3,2},{4,5},{5,4},{6,7},{7,6},{8,9},{9,8},{10,11... | collective-permute-start | bytes 73736 | tf_op jit(solution)/shard_map/ppermute | solution.py:220
  107.9 1.3 collective-permute-start.6
  133.5 2.3 %collective-permute-start.7 = (f32[48,128]{1,0:T(8,128)S(1)}, f32[48,128]{1,0:T(8,128)S(1)}, u32[]{:S(2)}, u32[]{:S(2)}) collective-permute-start(f32[48,128]{1,0:T(8,128)S(1)} %fusion.own), channel_id=1, source_target_pairs={{0,1},{1,0},{2,3},{3,2},{4,5},{5,4},{6,7},{7,6},{8,9},{9,8},{10,11... | collective-permute-start | bytes 73736 | tf_op jit(solution)/shard_map/ppermute | solution.py:220

commit v2 on v1

--- a/solution.py
+++ b/solution.py
@@ -36,19 +36,19 @@
     return high, (x - high.astype(F32)).astype(BF16)
 
 
-def image_of(scaled, high_ref, low_ref, core_ref, full, mine_ref, other_ref):
+def image_of(scaled, high_turned, low_turned, core_ref, full, mine_ref, other_ref):
     both = jnp.concatenate(split(scaled), axis=0)
-    total = dot(high_ref[...], both, NT) + dot(low_ref[...], both, NT)
+    total = dot(both, high_turned[...], NN) + dot(both, low_turned[...], NN)
+    total = total[:8] + total[8:]
     for j in range(TILES):
-        turned = total[j * LANES : (j + 1) * LANES, :].T
-        full[j * BANDS : (j + 1) * BANDS, :] = turned[:BANDS] + turned[8 : 8 + BANDS]
+        full[j * BANDS : (j + 1) * BANDS, :] = total[:BANDS, j * LANES : (j + 1) * LANES]
     full[TILES * BANDS :, :] = jnp.zeros((ROWS - TILES * BANDS, LANES), F32)
     first = core_ref[0:1, :] == 0
     for out, one, two in ((mine_ref, 0, HALF), (other_ref, HALF, 0)):
         out[...] = jnp.where(first, full[one : one + HALF, :], full[two : two + HALF, :])
 
 
-def first_kernel(core_ref, basis_hbm, pix_hbm, band_hbm, mag_hbm, var_hbm, mine_ref, other_ref, counts_ref, high_ref, low_ref,
+def first_kernel(core_ref, basis_hbm, pix_hbm, band_hbm, mag_hbm, var_hbm, mine_ref, other_ref, counts_ref, high_ref, low_ref, high_turned, low_turned,
                  raw, pix_ref, band_ref, mag_ref, var_ref, left, right, full, sems, obj_sems):
     obj_copies = [
         pltpu.make_async_copy(src, dst, obj_sems.at[i])
@@ -97,22 +97,28 @@
     for i, copy in enumerate(copies):
         copy.wait()
         cols = pl.ds(i * LANES, LANES)
-        for row in range(0, edge, 160):
-            rows = pl.ds(row, 160)
-            high_ref[rows, cols], low_ref[rows, cols] = split(raw[rows, cols])
-        tail = jnp.broadcast_to(raw[edge:NCOEF, cols], (WIDE - edge, LANES))
-        tail = jnp.where(lax.broadcasted_iota(jnp.int32, tail.shape, 0) == 0, tail, 0.0)
-        high_ref[edge:, cols], low_ref[edge:, cols] = split(tail)
-    image_of(weighted, high_ref, low_ref, core_ref, full, mine_ref, other_ref)
-
-
-def model_and_image(direction, wide, counts_ref, high_ref, low_ref, core_ref, full, mine_ref, other_ref):
+        for j in range(TILES):
+            rows = pl.ds(j * LANES, LANES)
+            if j < TILES - 1:
+                block = raw[rows, cols]
+            else:
+                size = WIDE - edge
+                tail = jnp.broadcast_to(raw[edge:NCOEF, cols], (size, LANES))
+                tail = jnp.where(lax.broadcasted_iota(jnp.int32, tail.shape, 0) == 0, tail, 0.0)
+                block = jnp.concatenate([raw[j * LANES : edge, cols], tail], axis=0)
+            high, low = split(block)
+            high_ref[rows, cols], low_ref[rows, cols] = high, low
+            high_turned[cols, rows], low_turned[cols, rows] = high.T, low.T
+    image_of(weighted, high_turned, low_turned, core_ref, full, mine_ref, other_ref)
+
+
+def model_and_image(direction, wide, counts_ref, high_ref, low_ref, high_turned, low_turned, core_ref, full, mine_ref, other_ref):
     wide[...] = jnp.zeros_like(wide)
     for j in range(TILES):
         wide[:BANDS, j * LANES : (j + 1) * LANES] = direction[j * BANDS : (j + 1) * BANDS, :]
     both = jnp.concatenate(split(wide[...]), axis=0)
     model = dot(both, high_ref[...], NN) + dot(both, low_ref[...], NN)
-    image_of(counts_ref[...] * (model[:8] + model[8:]), high_ref, low_ref, core_ref, full, mine_ref, other_ref)
+    image_of(counts_ref[...] * (model[:8] + model[8:]), high_turned, low_turned, core_ref, full, mine_ref, other_ref)
 
 
 def joined(core_ref, own_ref, near_ref):
@@ -125,12 +131,12 @@
     return jnp.sum(x, keepdims=True)
 
 
-def start_kernel(root, core_ref, own, near, counts_ref, high_ref, low_ref,
+def start_kernel(root, core_ref, own, near, counts_ref, high_ref, low_ref, high_turned, low_turned,
                  mine_ref, other_ref, res_ref, norm_ref, wide, full):
     right_side = joined(core_ref, own, near) / root
     res_ref[...] = right_side
     norm_ref[...] = jnp.broadcast_to(total_of(right_side * right_side), (8, LANES))
-    model_and_image(right_side, wide, counts_ref, high_ref, low_ref, core_ref, full, mine_ref, other_ref)
+    model_and_image(right_side, wide, counts_ref, high_ref, low_ref, high_turned, low_turned, core_ref, full, mine_ref, other_ref)
 
 
 def advance(pixels, whole, sol, res, direction, norm):
@@ -142,7 +148,7 @@
     return sol, res, res + norm_next / norm * direction, norm_next
 
 
-def step_kernel(pixels, core_ref, own, near, sol_ref, res_ref, dir_ref, norm_ref, counts_ref, high_ref, low_ref,
+def step_kernel(pixels, core_ref, own, near, sol_ref, res_ref, dir_ref, norm_ref, counts_ref, high_ref, low_ref, high_turned, low_turned,
                 mine_ref, other_ref, sol_out, res_out, dir_out, norm_out, wide, full):
     sol, res, direction, norm = advance(
         pixels, joined(core_ref, own, near), sol_ref[...], res_ref[...], dir_ref[...], norm_ref[0:1, 0:1]
@@ -151,7 +157,7 @@
     res_out[...] = res
     dir_out[...] = direction
     norm_out[...] = jnp.broadcast_to(norm, (8, LANES))
-    model_and_image(direction, wide, counts_ref, high_ref, low_ref, core_ref, full, mine_ref, other_ref)
+    model_and_image(direction, wide, counts_ref, high_ref, low_ref, high_turned, low_turned, core_ref, full, mine_ref, other_ref)
 
 
 def last_kernel(pixels, core_ref, own, near, sol_ref, res_ref, dir_ref, norm_ref, sol_out, res_out):
@@ -199,7 +205,8 @@
 def two_rounds():
     ys, zs, xs, pairs = range(SPAN["y"]), range(SPAN["z"]), range(SPAN["x"]), range(SPAN["y"] // 2)
     spread = sorted(zs, key=lambda z: (z % 2, z // 2 % 2, z))
-    one = [[device(y, z, x, 0) for y in ys for x in xs] for z in zs]
+    halves = sorted(xs, key=lambda x: (x % 2, x))
+    one = [[device(y, z, x, 0) for y in halves for x in halves] for z in zs]
     one += [[device(2 * pair + k, z, x, 1) for z in zs for k in (0, 1)] for x in xs for pair in pairs]
     two = [[device(y, z, x, 0) for z in spread] for y in ys for x in xs]
     two += [[device(y, z, x, 1) for x in xs for y in take] for z in zs for take in ((0, 3), (1, 2))]
@@ -226,11 +233,11 @@
     core = jnp.broadcast_to(lax.axis_index("c"), (8, LANES)).astype(jnp.int32)
     vec, half, norm_shape = shape(ROWS, LANES), shape(HALF, LANES), shape(8, LANES)
     scratch = [pltpu.VMEM((8, WIDE), F32), pltpu.VMEM((ROWS, LANES), F32)]
-    copied = shape(WIDE, PIX, kind=BF16)
-    mine, other, counts, high, low = call(
+    copied, turned = shape(WIDE, PIX, kind=BF16), shape(PIX, WIDE, kind=BF16)
+    mine, other, *fixed = call(
         first_kernel,
         "first",
-        [half, half, shape(8, PIX), copied, copied],
+        [half, half, shape(8, PIX), copied, copied, turned, turned],
         [VMEM] + [HBM] * 5,
         [
             pltpu.VMEM((NCOEF, PIX), F32),
@@ -246,13 +253,13 @@
         ],
     )(core, *[pltpu.with_memory_space_constraint(a, pltpu.HBM) for a in (basis.T, *objects)])
     mine, other, res, norm = call(
-        functools.partial(start_kernel, pixels**0.5), "start", [half, half, vec, norm_shape], [VMEM] * 6, scratch
-    )(core, *summed(mine, other), counts, high, low)
+        functools.partial(start_kernel, pixels**0.5), "start", [half, half, vec, norm_shape], [VMEM] * 8, scratch
+    )(core, *summed(mine, other), *fixed)
     sol, direction = jnp.zeros((ROWS, LANES), F32), res
     for _ in range(ITERS - 1):
         mine, other, sol, res, direction, norm = call(
-            functools.partial(step_kernel, pixels), "step", [half, half, vec, vec, vec, norm_shape], [VMEM] * 10, scratch
-        )(core, *summed(mine, other), sol, res, direction, norm, counts, high, low)
+            functools.partial(step_kernel, pixels), "step", [half, half, vec, vec, vec, norm_shape], [VMEM] * 12, scratch
+        )(core, *summed(mine, other), sol, res, direction, norm, *fixed)
     out = shape(BANDS, NCOEF)
     return tuple(
         call(functools.partial(last_kernel, pixels), "last", [out, out], [VMEM] * 7)(

time: 137 us -> 133 us (0.971)
  Pallas kernels: 15.8 us -> 13.7 us
    pallas_call x2, Pallas kernels: 5.12 us -> 3.7 us  [body(): call(functools.partial(step_kernel, pixels), 'step', [half, half, vec, ve...]
where the time goes in v2:
time: 133 us
  blocking collectives  102 us (77%)
  Pallas kernels  13.7 us (10%)
  starting transfers between devices  9.38 us (7%)
  waiting for transfers between devices  6.8 us (5%)
    all_to_all x8, blocking collectives, sent_to_all(): lax.all_to_all(sent, AXES, 0, 0, tiled=True, axis_index_groups=groups)  102 us
    pallas_call x1, Pallas kernels, body(): call(first_kernel, 'first', [half, half, shape(8, PIX), copied, copied, t...  7.59 us
    ppermute x4, starting transfers between devices, summed(): return (mine, lax.ppermute(mine, 'c', swap))  4.92 us
    ppermute x4, starting transfers between devices, summed(): mine = mine + lax.ppermute(other, 'c', swap)  4.45 us
    pallas_call x2, Pallas kernels, body(): call(functools.partial(step_kernel, pixels), 'step', [half, half, vec, ve...  3.7 us
    ppermute x4, waiting for transfers between devices, summed(): return (mine, lax.ppermute(mine, 'c', swap))  3.4 us
    ppermute x4, waiting for transfers between devices, summed(): mine = mine + lax.ppermute(other, 'c', swap)  3.4 us
  transfers between devices with their start and end apart: 8, of which 8 were waited for; matrix products, arithmetic and copies ran while one was open for 0% of the time, Pallas kernels for 0%

profile of v2, /device:TPU:1, one launch (start us, length us, event | category | flops | bytes accessed | tf_op | source)
XLA Modules:
  0.0 132.8 jit_solution(15290410336893905990)
XLA Ops:
  0.6 7.6 %first.1 = (f32[48,128]{1,0:T(8,128)S(1)}, f32[48,128]{1,0:T(8,128)S(1)}, f32[8,512]{1,0:T(8,128)S(1)}, bf16[2432,512]{1,0:T(8,128)(2,1)S(1)}, bf16[2432,512]{1,...) custom-call(s32[8,128]{1,0:T(8,128)S(1)} %broadcast_in_dim.28.core_ref, ...), custom_call_target="tpu_custom_call" | custom-call | tf_op jit(solution)/shard_map/first/pallas_call | solution.py:237
  8.2 3.3 %collective-permute-start = (f32[48,128]{1,0:T(8,128)S(1)}, f32[48,128]{1,0:T(8,128)S(1)}, u32[]{:S(2)}, u32[]{:S(2)}) collective-permute-start(f32[48,128]{1,0:T(8,128)S(1)} %get-tuple-element.26), channel_id=1, source_target_pairs={{0,1},{1,0},{2,3},{3,2},{4,5},{5,4},{6,7},{7,6},{8,9},{9,8},{10,11... | collective-permute-start | bytes 73736 | tf_op jit(solution)/shard_map/ppermute | solution.py:224
  11.5 0.8 collective-permute-done
  12.4 18.1 %all_to_all.40 = f32[16,48,128]{2,1,0:T(8,128)S(1)} all-to-all(f32[16,48,128]{2,1,0:T(8,128)S(1)} %broadcast_in_dim.29), channel_id=1, replica_groups={{0,4,2,6,128,132,130,134,64,68,66,70,192,196,194,198},{8,12,10,14,136,1..., dimensions={0} | all-to-all | bytes 786432 | tf_op jit(solution)/shard_map/all_to_all | solution.py:219
  30.6 12.0 %all_to_all.41 = f32[8,48,128]{2,1,0:T(8,128)S(1)} all-to-all(f32[8,48,128]{2,1,0:T(8,128)S(1)} %broadcast_in_dim.31), channel_id=1, replica_groups={{0,32,16,48,8,40,24,56},{2,34,18,50,10,42,26,58},{4,36,20,52,12,44,28,6..., dimensions={0} | all-to-all | bytes 393216 | tf_op jit(solution)/shard_map/all_to_all | solution.py:219
  42.6 1.4 %collective-permute-start.1 = (f32[48,128]{1,0:T(8,128)S(1)}, f32[48,128]{1,0:T(8,128)S(1)}, u32[]{:S(2)}, u32[]{:S(2)}) collective-permute-start(f32[48,128]{1,0:T(8,128)S(1)} %fusion.6.own), channel_id=1, source_target_pairs={{0,1},{1,0},{2,3},{3,2},{4,5},{5,4},{6,7},{7,6},{8,9},{9,8},{10,11... | collective-permute-start | bytes 73736 | tf_op jit(solution)/shard_map/ppermute | solution.py:227
  44.0 0.8 collective-permute-done.1.near
  44.9 1.5 %start.1 = (f32[48,128]{1,0:T(8,128)S(1)}, f32[48,128]{1,0:T(8,128)S(1)}, f32[96,128]{1,0:T(8,128)S(1)}, f32[8,128]{1,0:T(8,128)S(1)}) custom-call(s32[8,128]{1,0:T(8,128)S(1)} %broadcast_in_dim.28.core_ref, f32[48,128]{1,0:T(8,128)S(1)} %fusion.6.own, f32[48,128]{1,0:T(8,128)S(1)} %collective-permute-done.1.near, ...), custom_call_target="tpu_custom_call" | custom-call | tf_op jit(solution)/shard_map/start/pallas_call | solution.py:255
  46.4 0.4 collective-permute-start.2
  46.8 0.8 collective-permute-done.2
  47.7 14.1 %all_to_all.42 = f32[16,48,128]{2,1,0:T(8,128)S(1)} all-to-all(f32[16,48,128]{2,1,0:T(8,128)S(1)} %broadcast_in_dim.32), channel_id=1, replica_groups={{0,4,2,6,128,132,130,134,64,68,66,70,192,196,194,198},{8,12,10,14,136,1..., dimensions={0} | all-to-all | bytes 786432 | tf_op jit(solution)/shard_map/all_to_all | solution.py:219
  61.8 9.8 %all_to_all.43 = f32[8,48,128]{2,1,0:T(8,128)S(1)} all-to-all(f32[8,48,128]{2,1,0:T(8,128)S(1)} %broadcast_in_dim.68), channel_id=1, replica_groups={{0,32,16,48,8,40,24,56},{2,34,18,50,10,42,26,58},{4,36,20,52,12,44,28,6..., dimensions={0} | all-to-all | bytes 393216 | tf_op jit(solution)/shard_map/all_to_all | solution.py:219
  71.7 1.3 collective-permute-start.3
  72.9 0.8 collective-permute-done.3.near
  73.8 1.8 %step.2 = (f32[48,128]{1,0:T(8,128)S(1)}, f32[48,128]{1,0:T(8,128)S(1)}, f32[96,128]{1,0:T(8,128)S(1)}, f32[96,128]{1,0:T(8,128)S(1)}, f32[96,128]{1,0:T(8,128)S(1)}, /*index=5*/f32[8,128]{1,0:T(8,128)S(1)}) custom-call(s32[8,128]{1,0:T(8,128)S(1)} %broadcast_in_dim.28.core_ref, f32[48,128]{1,0:T(8,128)S(1)} %fusion.4.own, ...), custom_call_target="tpu_custom_call" | custom-call | tf_op jit(solution)/shard_map/step/pallas_call | solution.py:260
  75.6 0.4 collective-permute-start.4
  76.0 0.8 collective-permute-done.4
  76.9 14.0 %all_to_all.44 = f32[16,48,128]{2,1,0:T(8,128)S(1)} all-to-all(f32[16,48,128]{2,1,0:T(8,128)S(1)} %broadcast_in_dim.70), channel_id=1, replica_groups={{0,4,2,6,128,132,130,134,64,68,66,70,192,196,194,198},{8,12,10,14,136,1..., dimensions={0} | all-to-all | bytes 786432 | tf_op jit(solution)/shard_map/all_to_all | solution.py:219
  91.0 9.8 %all_to_all.45 = f32[8,48,128]{2,1,0:T(8,128)S(1)} all-to-all(f32[8,48,128]{2,1,0:T(8,128)S(1)} %broadcast_in_dim.72), channel_id=1, replica_groups={{0,32,16,48,8,40,24,56},{2,34,18,50,10,42,26,58},{4,36,20,52,12,44,28,6..., dimensions={0} | all-to-all | bytes 393216 | tf_op jit(solution)/shard_map/all_to_all | solution.py:219
  100.8 1.1 collective-permute-start.5
  102.0 0.8 collective-permute-done.5.near
  102.8 1.8 %step.3 = (f32[48,128]{1,0:T(8,128)S(1)}, f32[48,128]{1,0:T(8,128)S(1)}, f32[96,128]{1,0:T(8,128)S(1)}, f32[96,128]{1,0:T(8,128)S(1)}, f32[96,128]{1,0:T(8,128)S(1)}, /*index=5*/f32[8,128]{1,0:T(8,128)S(1)}) custom-call(s32[8,128]{1,0:T(8,128)S(1)} %broadcast_in_dim.28.core_ref, f32[48,128]{1,0:T(8,128)S(1)} %fusion.2.own, ...), custom_call_target="tpu_custom_call" | custom-call | tf_op jit(solution)/shard_map/step/pallas_call | solution.py:260
  104.7 0.4 collective-permute-start.6
  105.1 0.8 collective-permute-done.6
  105.9 14.2 %all_to_all.46 = f32[16,48,128]{2,1,0:T(8,128)S(1)} all-to-all(f32[16,48,128]{2,1,0:T(8,128)S(1)} %broadcast_in_dim.73), channel_id=1, replica_groups={{0,4,2,6,128,132,130,134,64,68,66,70,192,196,194,198},{8,12,10,14,136,1..., dimensions={0} | all-to-all | bytes 786432 | tf_op jit(solution)/shard_map/all_to_all | solution.py:219
  120.2 9.8 %all_to_all.47 = f32[8,48,128]{2,1,0:T(8,128)S(1)} all-to-all(f32[8,48,128]{2,1,0:T(8,128)S(1)} %broadcast_in_dim.75), channel_id=1, replica_groups={{0,32,16,48,8,40,24,56},{2,34,18,50,10,42,26,58},{4,36,20,52,12,44,28,6..., dimensions={0} | all-to-all | bytes 393216 | tf_op jit(solution)/shard_map/all_to_all | solution.py:219
  130.0 1.1 collective-permute-start.7
  131.1 0.8 collective-permute-done.7.near
  132.0 0.8 last.1
  (22 shorter events, 0.4 us)
Async XLA Ops:
  8.2 4.1 %collective-permute-start = (f32[48,128]{1,0:T(8,128)S(1)}, f32[48,128]{1,0:T(8,128)S(1)}, u32[]{:S(2)}, u32[]{:S(2)}) collective-permute-start(f32[48,128]{1,0:T(8,128)S(1)} %get-tuple-element.26), channel_id=1, source_target_pairs={{0,1},{1,0},{2,3},{3,2},{4,5},{5,4},{6,7},{7,6},{8,9},{9,8},{10,11... | collective-permute-start | bytes 73736 | tf_op jit(solution)/shard_map/ppermute | solution.py:224
  42.6 2.2 %collective-permute-start.1 = (f32[48,128]{1,0:T(8,128)S(1)}, f32[48,128]{1,0:T(8,128)S(1)}, u32[]{:S(2)}, u32[]{:S(2)}) collective-permute-start(f32[48,128]{1,0:T(8,128)S(1)} %fusion.6.own), channel_id=1, source_target_pairs={{0,1},{1,0},{2,3},{3,2},{4,5},{5,4},{6,7},{7,6},{8,9},{9,8},{10,11... | collective-permute-start | bytes 73736 | tf_op jit(solution)/shard_map/ppermute | solution.py:227
  46.4 1.2 collective-permute-start.2
  71.7 2.1 %collective-permute-start.3 = (f32[48,128]{1,0:T(8,128)S(1)}, f32[48,128]{1,0:T(8,128)S(1)}, u32[]{:S(2)}, u32[]{:S(2)}) collective-permute-start(f32[48,128]{1,0:T(8,128)S(1)} %fusion.4.own), channel_id=1, source_target_pairs={{0,1},{1,0},{2,3},{3,2},{4,5},{5,4},{6,7},{7,6},{8,9},{9,8},{10,11... | collective-permute-start | bytes 73736 | tf_op jit(solution)/shard_map/ppermute | solution.py:227
  75.6 1.2 collective-permute-start.4
  100.8 2.0 %collective-permute-start.5 = (f32[48,128]{1,0:T(8,128)S(1)}, f32[48,128]{1,0:T(8,128)S(1)}, u32[]{:S(2)}, u32[]{:S(2)}) collective-permute-start(f32[48,128]{1,0:T(8,128)S(1)} %fusion.2.own), channel_id=1, source_target_pairs={{0,1},{1,0},{2,3},{3,2},{4,5},{5,4},{6,7},{7,6},{8,9},{9,8},{10,11... | collective-permute-start | bytes 73736 | tf_op jit(solution)/shard_map/ppermute | solution.py:227
  104.7 1.2 collective-permute-start.6
  130.0 2.0 %collective-permute-start.7 = (f32[48,128]{1,0:T(8,128)S(1)}, f32[48,128]{1,0:T(8,128)S(1)}, u32[]{:S(2)}, u32[]{:S(2)}) collective-permute-start(f32[48,128]{1,0:T(8,128)S(1)} %fusion.own), channel_id=1, source_target_pairs={{0,1},{1,0},{2,3},{3,2},{4,5},{5,4},{6,7},{7,6},{8,9},{9,8},{10,11... | collective-permute-start | bytes 73736 | tf_op jit(solution)/shard_map/ppermute | solution.py:227

commit v3 on v2

--- a/solution.py
+++ b/solution.py
@@ -21,7 +21,6 @@
 ROWS = 96
 HALF = ROWS // 2
 OBJ_ROWS = 64
-STRIPES = PIX // LANES
 NT = (((1,), (1,)), ((), ()))
 NN = (((1,), (0,)), ((), ()))
 F32, BF16 = jnp.float32, jnp.bfloat16
@@ -49,20 +48,17 @@
 
 
 def first_kernel(core_ref, basis_hbm, pix_hbm, band_hbm, mag_hbm, var_hbm, mine_ref, other_ref, counts_ref, high_ref, low_ref, high_turned, low_turned,
-                 raw, pix_ref, band_ref, mag_ref, var_ref, left, right, full, sems, obj_sems):
+                 raw, pix_ref, band_ref, mag_ref, var_ref, left, right, full, sem, obj_sems):
     obj_copies = [
         pltpu.make_async_copy(src, dst, obj_sems.at[i])
         for i, (src, dst) in enumerate(((pix_hbm, pix_ref), (band_hbm, band_ref), (mag_hbm, mag_ref), (var_hbm, var_ref)))
     ]
-    copies = [
-        pltpu.make_async_copy(basis_hbm.at[:, pl.ds(i * LANES, LANES)], raw.at[:, pl.ds(i * LANES, LANES)], sems.at[i])
-        for i in range(STRIPES)
-    ]
-    for copy in obj_copies + copies:
+    basis_copy = pltpu.make_async_copy(basis_hbm, raw, sem)
+    for copy in (*obj_copies, basis_copy):
         copy.start()
-    group_no = lax.broadcasted_iota(jnp.int32, (32, LANES), 0)
-    lane_no = lax.broadcasted_iota(jnp.int32, (LANES, LANES), 0)
-
+    number = lax.broadcasted_iota(jnp.int32, (LANES, LANES), 0).astype(BF16)
+    sixteen = (16, LANES)
+    one, zero = jnp.ones(sixteen, BF16), jnp.zeros(sixteen, BF16)
     for copy in obj_copies:
         copy.wait()
 
@@ -72,18 +68,27 @@
         band = band_ref[pl.ds(at, 8), :]
         var = var_ref[pl.ds(at, 8), :]
         weight = var * mag_ref[pl.ds(at, 8), :]
-        group = lax.shift_right_logical(pix, 7) * 8 + band
-        low_pix = lax.bitwise_and(pix, LANES - 1)
+        group = (lax.shift_right_logical(pix, 7) * 8 + band).astype(F32)
+        low_pix = lax.bitwise_and(pix, LANES - 1).astype(F32)
         values = []
         for v in (var, weight):
             high = v.astype(BF16).astype(F32)
             values += [high, v - high]
+
+        def spread(rows, i):
+            return jnp.broadcast_to(rows[i : i + 1, :], sixteen).astype(BF16)
+
         for i in range(8):
-            mine = group_no == group[i : i + 1, :]
             to = pl.ds(pl.multiple_of(block * 8 * LANES, 8 * LANES) + i * LANES, LANES)
+            mine = spread(group, i)
+            where = [number[k : k + 16, :] == mine for k in (0, 16)]
             for k, v in enumerate(values):
-                left[k * 32 : (k + 1) * 32, to] = jnp.where(mine, v[i : i + 1, :], 0.0).astype(BF16)
-            right[:, to] = jnp.where(lane_no == low_pix[i : i + 1, :], 1.0, 0.0).astype(BF16)
+                v = spread(v, i)
+                for h in (0, 1):
+                    left[k * 32 + h * 16 : k * 32 + h * 16 + 16, to] = jnp.where(where[h], v, zero)
+            pixel = spread(low_pix, i)
+            for k in range(0, LANES, 16):
+                right[k : k + 16, to] = jnp.where(number[k : k + 16, :] == pixel, one, zero)
         return carry
 
     lax.fori_loop(0, OBJ_ROWS // 8, objects, 0)
@@ -94,8 +99,8 @@
     ]
     counts_ref[...] = counts
     edge = NCOEF // 16 * 16
-    for i, copy in enumerate(copies):
-        copy.wait()
+    basis_copy.wait()
+    for i in range(PIX // LANES):
         cols = pl.ds(i * LANES, LANES)
         for j in range(TILES):
             rows = pl.ds(j * LANES, LANES)
@@ -248,7 +253,7 @@
             pltpu.VMEM((128, OBJ_ROWS * LANES), BF16),
             pltpu.VMEM((128, OBJ_ROWS * LANES), BF16),
             pltpu.VMEM((ROWS, LANES), F32),
-            pltpu.SemaphoreType.DMA((STRIPES,)),
+            pltpu.SemaphoreType.DMA,
             pltpu.SemaphoreType.DMA((4,)),
         ],
     )(core, *[pltpu.with_memory_space_constraint(a, pltpu.HBM) for a in (basis.T, *objects)])

time: 133 us -> 131 us (0.985)
  Pallas kernels: 13.7 us -> 12 us
    pallas_call x1, Pallas kernels: 7.59 us -> 5.87 us  [body(): call(first_kernel, 'first', [half, half, shape(8, PIX), copied, copied, t...]
where the time goes in v3:
time: 131 us
  blocking collectives  102 us (78%)
  Pallas kernels  12 us (9%)
  starting transfers between devices  9.38 us (7%)
  waiting for transfers between devices  6.8 us (5%)
    all_to_all x8, blocking collectives, sent_to_all(): lax.all_to_all(sent, AXES, 0, 0, tiled=True, axis_index_groups=groups)  102 us
    pallas_call x1, Pallas kernels, body(): call(first_kernel, 'first', [half, half, shape(8, PIX), copied, copied, t...  5.87 us
    ppermute x4, starting transfers between devices, summed(): return (mine, lax.ppermute(mine, 'c', swap))  4.92 us
    ppermute x4, starting transfers between devices, summed(): mine = mine + lax.ppermute(other, 'c', swap)  4.45 us
    pallas_call x2, Pallas kernels, body(): call(functools.partial(step_kernel, pixels), 'step', [half, half, vec, ve...  3.7 us
    ppermute x4, waiting for transfers between devices, summed(): mine = mine + lax.ppermute(other, 'c', swap)  3.4 us
    ppermute x4, waiting for transfers between devices, summed(): return (mine, lax.ppermute(mine, 'c', swap))  3.4 us
  transfers between devices with their start and end apart: 8, of which 8 were waited for; matrix products, arithmetic and copies ran while one was open for 0% of the time, Pallas kernels for 0%

profile of v3, /device:TPU:1, one launch (start us, length us, event | category | flops | bytes accessed | tf_op | source)
XLA Modules:
  0.0 131.1 jit_solution(3909758673744030379)
XLA Ops:
  0.6 5.9 %first.1 = (f32[48,128]{1,0:T(8,128)S(1)}, f32[48,128]{1,0:T(8,128)S(1)}, f32[8,512]{1,0:T(8,128)S(1)}, bf16[2432,512]{1,0:T(8,128)(2,1)S(1)}, bf16[2432,512]{1,...) custom-call(s32[8,128]{1,0:T(8,128)S(1)} %broadcast_in_dim.28.core_ref, ...), custom_call_target="tpu_custom_call" | custom-call | tf_op jit(solution)/shard_map/first/pallas_call | solution.py:242
  6.5 3.3 %collective-permute-start = (f32[48,128]{1,0:T(8,128)S(1)}, f32[48,128]{1,0:T(8,128)S(1)}, u32[]{:S(2)}, u32[]{:S(2)}) collective-permute-start(f32[48,128]{1,0:T(8,128)S(1)} %get-tuple-element.26), channel_id=1, source_target_pairs={{0,1},{1,0},{2,3},{3,2},{4,5},{5,4},{6,7},{7,6},{8,9},{9,8},{10,11... | collective-permute-start | bytes 73736 | tf_op jit(solution)/shard_map/ppermute | solution.py:229
  9.8 0.8 collective-permute-done
  10.7 18.1 %all_to_all.40 = f32[16,48,128]{2,1,0:T(8,128)S(1)} all-to-all(f32[16,48,128]{2,1,0:T(8,128)S(1)} %broadcast_in_dim.29), channel_id=1, replica_groups={{0,4,2,6,128,132,130,134,64,68,66,70,192,196,194,198},{8,12,10,14,136,1..., dimensions={0} | all-to-all | bytes 786432 | tf_op jit(solution)/shard_map/all_to_all | solution.py:224
  28.9 12.0 %all_to_all.41 = f32[8,48,128]{2,1,0:T(8,128)S(1)} all-to-all(f32[8,48,128]{2,1,0:T(8,128)S(1)} %broadcast_in_dim.31), channel_id=1, replica_groups={{0,32,16,48,8,40,24,56},{2,34,18,50,10,42,26,58},{4,36,20,52,12,44,28,6..., dimensions={0} | all-to-all | bytes 393216 | tf_op jit(solution)/shard_map/all_to_all | solution.py:224
  40.9 1.4 %collective-permute-start.1 = (f32[48,128]{1,0:T(8,128)S(1)}, f32[48,128]{1,0:T(8,128)S(1)}, u32[]{:S(2)}, u32[]{:S(2)}) collective-permute-start(f32[48,128]{1,0:T(8,128)S(1)} %fusion.6.own), channel_id=1, source_target_pairs={{0,1},{1,0},{2,3},{3,2},{4,5},{5,4},{6,7},{7,6},{8,9},{9,8},{10,11... | collective-permute-start | bytes 73736 | tf_op jit(solution)/shard_map/ppermute | solution.py:232
  42.3 0.8 collective-permute-done.1.near
  43.1 1.5 %start.1 = (f32[48,128]{1,0:T(8,128)S(1)}, f32[48,128]{1,0:T(8,128)S(1)}, f32[96,128]{1,0:T(8,128)S(1)}, f32[8,128]{1,0:T(8,128)S(1)}) custom-call(s32[8,128]{1,0:T(8,128)S(1)} %broadcast_in_dim.28.core_ref, f32[48,128]{1,0:T(8,128)S(1)} %fusion.6.own, f32[48,128]{1,0:T(8,128)S(1)} %collective-permute-done.1.near, ...), custom_call_target="tpu_custom_call" | custom-call | tf_op jit(solution)/shard_map/start/pallas_call | solution.py:260
  44.7 0.4 collective-permute-start.2
  45.1 0.8 collective-permute-done.2
  46.0 14.1 %all_to_all.42 = f32[16,48,128]{2,1,0:T(8,128)S(1)} all-to-all(f32[16,48,128]{2,1,0:T(8,128)S(1)} %broadcast_in_dim.32), channel_id=1, replica_groups={{0,4,2,6,128,132,130,134,64,68,66,70,192,196,194,198},{8,12,10,14,136,1..., dimensions={0} | all-to-all | bytes 786432 | tf_op jit(solution)/shard_map/all_to_all | solution.py:224
  60.1 9.8 %all_to_all.43 = f32[8,48,128]{2,1,0:T(8,128)S(1)} all-to-all(f32[8,48,128]{2,1,0:T(8,128)S(1)} %broadcast_in_dim.68), channel_id=1, replica_groups={{0,32,16,48,8,40,24,56},{2,34,18,50,10,42,26,58},{4,36,20,52,12,44,28,6..., dimensions={0} | all-to-all | bytes 393216 | tf_op jit(solution)/shard_map/all_to_all | solution.py:224
  69.9 1.3 collective-permute-start.3
  71.2 0.8 collective-permute-done.3.near
  72.1 1.8 %step.2 = (f32[48,128]{1,0:T(8,128)S(1)}, f32[48,128]{1,0:T(8,128)S(1)}, f32[96,128]{1,0:T(8,128)S(1)}, f32[96,128]{1,0:T(8,128)S(1)}, f32[96,128]{1,0:T(8,128)S(1)}, /*index=5*/f32[8,128]{1,0:T(8,128)S(1)}) custom-call(s32[8,128]{1,0:T(8,128)S(1)} %broadcast_in_dim.28.core_ref, f32[48,128]{1,0:T(8,128)S(1)} %fusion.4.own, ...), custom_call_target="tpu_custom_call" | custom-call | tf_op jit(solution)/shard_map/step/pallas_call | solution.py:265
  73.9 0.4 collective-permute-start.4
  74.3 0.8 collective-permute-done.4
  75.2 14.0 %all_to_all.44 = f32[16,48,128]{2,1,0:T(8,128)S(1)} all-to-all(f32[16,48,128]{2,1,0:T(8,128)S(1)} %broadcast_in_dim.70), channel_id=1, replica_groups={{0,4,2,6,128,132,130,134,64,68,66,70,192,196,194,198},{8,12,10,14,136,1..., dimensions={0} | all-to-all | bytes 786432 | tf_op jit(solution)/shard_map/all_to_all | solution.py:224
  89.3 9.8 %all_to_all.45 = f32[8,48,128]{2,1,0:T(8,128)S(1)} all-to-all(f32[8,48,128]{2,1,0:T(8,128)S(1)} %broadcast_in_dim.72), channel_id=1, replica_groups={{0,32,16,48,8,40,24,56},{2,34,18,50,10,42,26,58},{4,36,20,52,12,44,28,6..., dimensions={0} | all-to-all | bytes 393216 | tf_op jit(solution)/shard_map/all_to_all | solution.py:224
  99.1 1.1 collective-permute-start.5
  100.3 0.8 collective-permute-done.5.near
  101.1 1.8 %step.3 = (f32[48,128]{1,0:T(8,128)S(1)}, f32[48,128]{1,0:T(8,128)S(1)}, f32[96,128]{1,0:T(8,128)S(1)}, f32[96,128]{1,0:T(8,128)S(1)}, f32[96,128]{1,0:T(8,128)S(1)}, /*index=5*/f32[8,128]{1,0:T(8,128)S(1)}) custom-call(s32[8,128]{1,0:T(8,128)S(1)} %broadcast_in_dim.28.core_ref, f32[48,128]{1,0:T(8,128)S(1)} %fusion.2.own, ...), custom_call_target="tpu_custom_call" | custom-call | tf_op jit(solution)/shard_map/step/pallas_call | solution.py:265
  103.0 0.4 collective-permute-start.6
  103.3 0.8 collective-permute-done.6
  104.2 14.2 %all_to_all.46 = f32[16,48,128]{2,1,0:T(8,128)S(1)} all-to-all(f32[16,48,128]{2,1,0:T(8,128)S(1)} %broadcast_in_dim.73), channel_id=1, replica_groups={{0,4,2,6,128,132,130,134,64,68,66,70,192,196,194,198},{8,12,10,14,136,1..., dimensions={0} | all-to-all | bytes 786432 | tf_op jit(solution)/shard_map/all_to_all | solution.py:224
  118.5 9.8 %all_to_all.47 = f32[8,48,128]{2,1,0:T(8,128)S(1)} all-to-all(f32[8,48,128]{2,1,0:T(8,128)S(1)} %broadcast_in_dim.75), channel_id=1, replica_groups={{0,32,16,48,8,40,24,56},{2,34,18,50,10,42,26,58},{4,36,20,52,12,44,28,6..., dimensions={0} | all-to-all | bytes 393216 | tf_op jit(solution)/shard_map/all_to_all | solution.py:224
  128.3 1.1 collective-permute-start.7
  129.4 0.8 collective-permute-done.7.near
  130.3 0.8 last.1
  (22 shorter events, 0.4 us)
Async XLA Ops:
  6.5 4.1 %collective-permute-start = (f32[48,128]{1,0:T(8,128)S(1)}, f32[48,128]{1,0:T(8,128)S(1)}, u32[]{:S(2)}, u32[]{:S(2)}) collective-permute-start(f32[48,128]{1,0:T(8,128)S(1)} %get-tuple-element.26), channel_id=1, source_target_pairs={{0,1},{1,0},{2,3},{3,2},{4,5},{5,4},{6,7},{7,6},{8,9},{9,8},{10,11... | collective-permute-start | bytes 73736 | tf_op jit(solution)/shard_map/ppermute | solution.py:229
  40.9 2.2 %collective-permute-start.1 = (f32[48,128]{1,0:T(8,128)S(1)}, f32[48,128]{1,0:T(8,128)S(1)}, u32[]{:S(2)}, u32[]{:S(2)}) collective-permute-start(f32[48,128]{1,0:T(8,128)S(1)} %fusion.6.own), channel_id=1, source_target_pairs={{0,1},{1,0},{2,3},{3,2},{4,5},{5,4},{6,7},{7,6},{8,9},{9,8},{10,11... | collective-permute-start | bytes 73736 | tf_op jit(solution)/shard_map/ppermute | solution.py:232
  44.7 1.2 collective-permute-start.2
  69.9 2.1 %collective-permute-start.3 = (f32[48,128]{1,0:T(8,128)S(1)}, f32[48,128]{1,0:T(8,128)S(1)}, u32[]{:S(2)}, u32[]{:S(2)}) collective-permute-start(f32[48,128]{1,0:T(8,128)S(1)} %fusion.4.own), channel_id=1, source_target_pairs={{0,1},{1,0},{2,3},{3,2},{4,5},{5,4},{6,7},{7,6},{8,9},{9,8},{10,11... | collective-permute-start | bytes 73736 | tf_op jit(solution)/shard_map/ppermute | solution.py:232
  73.9 1.2 collective-permute-start.4
  99.1 2.0 %collective-permute-start.5 = (f32[48,128]{1,0:T(8,128)S(1)}, f32[48,128]{1,0:T(8,128)S(1)}, u32[]{:S(2)}, u32[]{:S(2)}) collective-permute-start(f32[48,128]{1,0:T(8,128)S(1)} %fusion.2.own), channel_id=1, source_target_pairs={{0,1},{1,0},{2,3},{3,2},{4,5},{5,4},{6,7},{7,6},{8,9},{9,8},{10,11... | collective-permute-start | bytes 73736 | tf_op jit(solution)/shard_map/ppermute | solution.py:232
  103.0 1.2 collective-permute-start.6
  128.3 2.0 %collective-permute-start.7 = (f32[48,128]{1,0:T(8,128)S(1)}, f32[48,128]{1,0:T(8,128)S(1)}, u32[]{:S(2)}, u32[]{:S(2)}) collective-permute-start(f32[48,128]{1,0:T(8,128)S(1)} %fusion.own), channel_id=1, source_target_pairs={{0,1},{1,0},{2,3},{3,2},{4,5},{5,4},{6,7},{7,6},{8,9},{9,8},{10,11... | collective-permute-start | bytes 73736 | tf_op jit(solution)/shard_map/ppermute | solution.py:232

commit v4 on v3

--- a/solution.py
+++ b/solution.py
@@ -209,7 +209,7 @@
 
 def two_rounds():
     ys, zs, xs, pairs = range(SPAN["y"]), range(SPAN["z"]), range(SPAN["x"]), range(SPAN["y"] // 2)
-    spread = sorted(zs, key=lambda z: (z % 2, z // 2 % 2, z))
+    spread = sorted(zs, key=lambda z: (z % 4, z))
     halves = sorted(xs, key=lambda x: (x % 2, x))
     one = [[device(y, z, x, 0) for y in halves for x in halves] for z in zs]
     one += [[device(2 * pair + k, z, x, 1) for z in zs for k in (0, 1)] for x in xs for pair in pairs]

time: 131 us -> 131 us (level)
  no operation moved by 1% of the time
where the time goes in v4:
time: 131 us
  blocking collectives  102 us (78%)
  Pallas kernels  12 us (9%)
  starting transfers between devices  8.9 us (7%)
  waiting for transfers between devices  6.8 us (5%)
    all_to_all x8, blocking collectives, sent_to_all(): lax.all_to_all(sent, AXES, 0, 0, tiled=True, axis_index_groups=groups)  102 us
    pallas_call x1, Pallas kernels, body(): call(first_kernel, 'first', [half, half, shape(8, PIX), copied, copied, t...  5.87 us
    ppermute x4, starting transfers between devices, summed(): mine = mine + lax.ppermute(other, 'c', swap)  4.45 us
    ppermute x4, starting transfers between devices, summed(): return (mine, lax.ppermute(mine, 'c', swap))  4.44 us
    pallas_call x2, Pallas kernels, body(): call(functools.partial(step_kernel, pixels), 'step', [half, half, vec, ve...  3.7 us
    ppermute x4, waiting for transfers between devices, summed(): return (mine, lax.ppermute(mine, 'c', swap))  3.4 us
    ppermute x4, waiting for transfers between devices, summed(): mine = mine + lax.ppermute(other, 'c', swap)  3.4 us
  transfers between devices with their start and end apart: 8, of which 8 were waited for; matrix products, arithmetic and copies ran while one was open for 0% of the time, Pallas kernels for 0%

profile of v4, /device:TPU:1, one launch (start us, length us, event | category | flops | bytes accessed | tf_op | source)
XLA Modules:
  0.0 130.9 jit_solution(15133729666835156262)
XLA Ops:
  0.6 5.9 %first.1 = (f32[48,128]{1,0:T(8,128)S(1)}, f32[48,128]{1,0:T(8,128)S(1)}, f32[8,512]{1,0:T(8,128)S(1)}, bf16[2432,512]{1,0:T(8,128)(2,1)S(1)}, bf16[2432,512]{1,...) custom-call(s32[8,128]{1,0:T(8,128)S(1)} %broadcast_in_dim.28.core_ref, ...), custom_call_target="tpu_custom_call" | custom-call | tf_op jit(solution)/shard_map/first/pallas_call | solution.py:242
  6.5 3.3 %collective-permute-start = (f32[48,128]{1,0:T(8,128)S(1)}, f32[48,128]{1,0:T(8,128)S(1)}, u32[]{:S(2)}, u32[]{:S(2)}) collective-permute-start(f32[48,128]{1,0:T(8,128)S(1)} %get-tuple-element.26), channel_id=1, source_target_pairs={{0,1},{1,0},{2,3},{3,2},{4,5},{5,4},{6,7},{7,6},{8,9},{9,8},{10,11... | collective-permute-start | bytes 73736 | tf_op jit(solution)/shard_map/ppermute | solution.py:229
  9.8 0.8 collective-permute-done
  10.7 18.1 %all_to_all.40 = f32[16,48,128]{2,1,0:T(8,128)S(1)} all-to-all(f32[16,48,128]{2,1,0:T(8,128)S(1)} %broadcast_in_dim.29), channel_id=1, replica_groups={{0,4,2,6,128,132,130,134,64,68,66,70,192,196,194,198},{8,12,10,14,136,1..., dimensions={0} | all-to-all | bytes 786432 | tf_op jit(solution)/shard_map/all_to_all | solution.py:224
  28.9 12.1 %all_to_all.41 = f32[8,48,128]{2,1,0:T(8,128)S(1)} all-to-all(f32[8,48,128]{2,1,0:T(8,128)S(1)} %broadcast_in_dim.31), channel_id=1, replica_groups={{0,32,8,40,16,48,24,56},{2,34,10,42,18,50,26,58},{4,36,12,44,20,52,28,6..., dimensions={0} | all-to-all | bytes 393216 | tf_op jit(solution)/shard_map/all_to_all | solution.py:224
  41.0 1.3 collective-permute-start.1
  42.3 0.8 collective-permute-done.1.near
  43.2 1.5 %start.1 = (f32[48,128]{1,0:T(8,128)S(1)}, f32[48,128]{1,0:T(8,128)S(1)}, f32[96,128]{1,0:T(8,128)S(1)}, f32[8,128]{1,0:T(8,128)S(1)}) custom-call(s32[8,128]{1,0:T(8,128)S(1)} %broadcast_in_dim.28.core_ref, f32[48,128]{1,0:T(8,128)S(1)} %fusion.6.own, f32[48,128]{1,0:T(8,128)S(1)} %collective-permute-done.1.near, ...), custom_call_target="tpu_custom_call" | custom-call | tf_op jit(solution)/shard_map/start/pallas_call | solution.py:260
  44.7 0.4 collective-permute-start.2
  45.1 0.8 collective-permute-done.2
  46.0 14.1 %all_to_all.42 = f32[16,48,128]{2,1,0:T(8,128)S(1)} all-to-all(f32[16,48,128]{2,1,0:T(8,128)S(1)} %broadcast_in_dim.32), channel_id=1, replica_groups={{0,4,2,6,128,132,130,134,64,68,66,70,192,196,194,198},{8,12,10,14,136,1..., dimensions={0} | all-to-all | bytes 786432 | tf_op jit(solution)/shard_map/all_to_all | solution.py:224
  60.1 10.1 %all_to_all.43 = f32[8,48,128]{2,1,0:T(8,128)S(1)} all-to-all(f32[8,48,128]{2,1,0:T(8,128)S(1)} %broadcast_in_dim.68), channel_id=1, replica_groups={{0,32,8,40,16,48,24,56},{2,34,10,42,18,50,26,58},{4,36,12,44,20,52,28,6..., dimensions={0} | all-to-all | bytes 393216 | tf_op jit(solution)/shard_map/all_to_all | solution.py:224
  70.2 0.8 collective-permute-start.3
  71.0 0.8 collective-permute-done.3.near
  71.9 1.8 %step.2 = (f32[48,128]{1,0:T(8,128)S(1)}, f32[48,128]{1,0:T(8,128)S(1)}, f32[96,128]{1,0:T(8,128)S(1)}, f32[96,128]{1,0:T(8,128)S(1)}, f32[96,128]{1,0:T(8,128)S(1)}, /*index=5*/f32[8,128]{1,0:T(8,128)S(1)}) custom-call(s32[8,128]{1,0:T(8,128)S(1)} %broadcast_in_dim.28.core_ref, f32[48,128]{1,0:T(8,128)S(1)} %fusion.4.own, ...), custom_call_target="tpu_custom_call" | custom-call | tf_op jit(solution)/shard_map/step/pallas_call | solution.py:265
  73.7 0.4 collective-permute-start.4
  74.1 0.8 collective-permute-done.4
  75.0 14.2 %all_to_all.44 = f32[16,48,128]{2,1,0:T(8,128)S(1)} all-to-all(f32[16,48,128]{2,1,0:T(8,128)S(1)} %broadcast_in_dim.70), channel_id=1, replica_groups={{0,4,2,6,128,132,130,134,64,68,66,70,192,196,194,198},{8,12,10,14,136,1..., dimensions={0} | all-to-all | bytes 786432 | tf_op jit(solution)/shard_map/all_to_all | solution.py:224
  89.2 9.7 %all_to_all.45 = f32[8,48,128]{2,1,0:T(8,128)S(1)} all-to-all(f32[8,48,128]{2,1,0:T(8,128)S(1)} %broadcast_in_dim.72), channel_id=1, replica_groups={{0,32,8,40,16,48,24,56},{2,34,10,42,18,50,26,58},{4,36,12,44,20,52,28,6..., dimensions={0} | all-to-all | bytes 393216 | tf_op jit(solution)/shard_map/all_to_all | solution.py:224
  99.0 1.2 collective-permute-start.5
  100.2 0.8 collective-permute-done.5.near
  101.0 1.8 %step.3 = (f32[48,128]{1,0:T(8,128)S(1)}, f32[48,128]{1,0:T(8,128)S(1)}, f32[96,128]{1,0:T(8,128)S(1)}, f32[96,128]{1,0:T(8,128)S(1)}, f32[96,128]{1,0:T(8,128)S(1)}, /*index=5*/f32[8,128]{1,0:T(8,128)S(1)}) custom-call(s32[8,128]{1,0:T(8,128)S(1)} %broadcast_in_dim.28.core_ref, f32[48,128]{1,0:T(8,128)S(1)} %fusion.2.own, ...), custom_call_target="tpu_custom_call" | custom-call | tf_op jit(solution)/shard_map/step/pallas_call | solution.py:265
  102.9 0.4 collective-permute-start.6
  103.3 0.8 collective-permute-done.6
  104.1 14.0 %all_to_all.46 = f32[16,48,128]{2,1,0:T(8,128)S(1)} all-to-all(f32[16,48,128]{2,1,0:T(8,128)S(1)} %broadcast_in_dim.73), channel_id=1, replica_groups={{0,4,2,6,128,132,130,134,64,68,66,70,192,196,194,198},{8,12,10,14,136,1..., dimensions={0} | all-to-all | bytes 786432 | tf_op jit(solution)/shard_map/all_to_all | solution.py:224
  118.2 9.8 %all_to_all.47 = f32[8,48,128]{2,1,0:T(8,128)S(1)} all-to-all(f32[8,48,128]{2,1,0:T(8,128)S(1)} %broadcast_in_dim.75), channel_id=1, replica_groups={{0,32,8,40,16,48,24,56},{2,34,10,42,18,50,26,58},{4,36,12,44,20,52,28,6..., dimensions={0} | all-to-all | bytes 393216 | tf_op jit(solution)/shard_map/all_to_all | solution.py:224
  128.0 1.2 collective-permute-start.7
  129.2 0.8 collective-permute-done.7.near
  130.1 0.8 last.1
  (22 shorter events, 0.4 us)
Async XLA Ops:
  6.5 4.1 %collective-permute-start = (f32[48,128]{1,0:T(8,128)S(1)}, f32[48,128]{1,0:T(8,128)S(1)}, u32[]{:S(2)}, u32[]{:S(2)}) collective-permute-start(f32[48,128]{1,0:T(8,128)S(1)} %get-tuple-element.26), channel_id=1, source_target_pairs={{0,1},{1,0},{2,3},{3,2},{4,5},{5,4},{6,7},{7,6},{8,9},{9,8},{10,11... | collective-permute-start | bytes 73736 | tf_op jit(solution)/shard_map/ppermute | solution.py:229
  41.0 2.1 %collective-permute-start.1 = (f32[48,128]{1,0:T(8,128)S(1)}, f32[48,128]{1,0:T(8,128)S(1)}, u32[]{:S(2)}, u32[]{:S(2)}) collective-permute-start(f32[48,128]{1,0:T(8,128)S(1)} %fusion.6.own), channel_id=1, source_target_pairs={{0,1},{1,0},{2,3},{3,2},{4,5},{5,4},{6,7},{7,6},{8,9},{9,8},{10,11... | collective-permute-start | bytes 73736 | tf_op jit(solution)/shard_map/ppermute | solution.py:232
  44.7 1.2 collective-permute-start.2
  70.2 1.6 %collective-permute-start.3 = (f32[48,128]{1,0:T(8,128)S(1)}, f32[48,128]{1,0:T(8,128)S(1)}, u32[]{:S(2)}, u32[]{:S(2)}) collective-permute-start(f32[48,128]{1,0:T(8,128)S(1)} %fusion.4.own), channel_id=1, source_target_pairs={{0,1},{1,0},{2,3},{3,2},{4,5},{5,4},{6,7},{7,6},{8,9},{9,8},{10,11... | collective-permute-start | bytes 73736 | tf_op jit(solution)/shard_map/ppermute | solution.py:232
  73.7 1.2 collective-permute-start.4
  99.0 2.0 %collective-permute-start.5 = (f32[48,128]{1,0:T(8,128)S(1)}, f32[48,128]{1,0:T(8,128)S(1)}, u32[]{:S(2)}, u32[]{:S(2)}) collective-permute-start(f32[48,128]{1,0:T(8,128)S(1)} %fusion.2.own), channel_id=1, source_target_pairs={{0,1},{1,0},{2,3},{3,2},{4,5},{5,4},{6,7},{7,6},{8,9},{9,8},{10,11... | collective-permute-start | bytes 73736 | tf_op jit(solution)/shard_map/ppermute | solution.py:232
  102.9 1.2 collective-permute-start.6
  128.0 2.0 %collective-permute-start.7 = (f32[48,128]{1,0:T(8,128)S(1)}, f32[48,128]{1,0:T(8,128)S(1)}, u32[]{:S(2)}, u32[]{:S(2)}) collective-permute-start(f32[48,128]{1,0:T(8,128)S(1)} %fusion.own), channel_id=1, source_target_pairs={{0,1},{1,0},{2,3},{3,2},{4,5},{5,4},{6,7},{7,6},{8,9},{9,8},{10,11... | collective-permute-start | bytes 73736 | tf_op jit(solution)/shard_map/ppermute | solution.py:232
